TPU v7x, 8 devices: a whole 2x2x1 slice. The times are simulated.
8 devices in a mesh: member: 1 (over z), lon: 2 (over y), lat: 4 (over x, core).
Axes of the slice: x: 2, y: 2, z: 1, core: 2. Of those that a mesh axis runs over, the one named last changes fastest.
Arguments:
- grid_field: float32 [4, 256, 256, 512], P('member', None, 'lat', 'lon')
- mix_weight: bfloat16 [256, 256, 256, 2], replicated
Outputs:
- output: float32 [4, 256, 256, 512], P('member', None, 'lat', 'lon')
All inputs are finite; a program needn't handle non-finite values.
Results may differ from a plain program's by a relative error of at most 0.00431334.
Values are sent between devices in bfloat16 or wider.
A program may use at most 1 GiB of HBM per device.

v0:
```python
import functools
import math
import numpy as np
import jax
import jax.numpy as jnp
from jax import lax
from jax.experimental import pallas as pl
from jax.experimental.pallas import tpu as pltpu
from jax.sharding import PartitionSpec as P


BF = jnp.bfloat16
F32 = jnp.float32
LB = 16
HALVES = ((16, 48), (32, 16, 16))
MB = 32
PAD = LB + 1
MG = 64
NV = 4
MIX = ((1, 0), (3,), (2,))
NT = (((1,), (1,)), ((), ()))
TN = (((0,), (0,)), ((), ()))


def legendre_tables(n_lat, n_lon, n_deg):
    t = (np.arange(n_lat) + 0.5) * (math.pi / n_lat)
    x = np.cos(t)
    m = np.arange(n_deg)
    steps = np.concatenate([[0.0], np.cumsum(0.5 * np.log((2.0 * m[1:] + 1.0) / (2.0 * m[1:])))])
    diag = np.exp(0.5 * math.log(0.5) + steps[:, None] + m[:, None] * np.log(np.sin(t))[None, :])
    tab = np.zeros((n_deg, n_deg, n_lat))
    mm = m[:, None].astype(np.float64)
    prev1 = np.zeros((n_deg, n_lat))
    prev2 = np.zeros((n_deg, n_lat))
    for l in range(n_deg):
        a = np.sqrt((4.0 * l * l - 1.0) / np.maximum(l * l - mm * mm, 1.0)) if l > 0 else np.ones_like(mm)
        b = np.sqrt(np.maximum((l - 1.0) ** 2 - mm * mm, 0.0) / max(4.0 * (l - 1.0) ** 2 - 1.0, 1.0))
        cur = np.where(mm < l, a * (x[None, :] * prev1 - b * prev2), 0.0)
        cur[l] = diag[l]
        tab[:, l, :] = cur
        prev2 = prev1
        prev1 = cur
    n = np.arange(1, n_lat // 2 + 1)
    series = np.sum(np.cos(2.0 * t[:, None] * n[None, :]) / (4.0 * n * n - 1.0), axis=1)
    w = (2.0 / n_lat) * (1.0 - 2.0 * series)

    def pack(p):
        p = p.astype(np.float32).astype(BF).reshape(n_deg, n_deg // (2 * LB), 2, LB, n_lat)
        p = p.transpose(0, 2, 1, 3, 4).reshape(n_deg, 2, NV, n_deg // 2 // NV, n_lat)
        return [np.ascontiguousarray(p[:MG * (v + 1), :, v]) for v in range(NV)]

    return pack(tab * (w / n_lon)), pack(tab)


def dft_tables(n_lon, n_deg):
    ang = ((np.arange(n_deg)[:, None] * np.arange(n_lon)[None, :]) % n_lon) * (2.0 * math.pi / n_lon)
    c_m = np.where(np.arange(n_deg) == 0, 1.0, 2.0)[:, None, None]
    fwd = np.stack([np.cos(ang), -np.sin(ang)], axis=1)

    def pack(p):
        p = p.astype(np.float32).astype(BF).reshape(2 * n_deg, 2, n_lon // 2)
        return np.ascontiguousarray(np.stack([p, p[:, ::-1]])).reshape(2, 2 * n_deg, n_lon)

    return pack(fwd), pack(c_m * fwd)


def cast_kernel(s_ref, *refs):
    n = len(refs) // 2
    for t in range(n):
        refs[n + t][...] = refs[t][0, 0, 0].astype(BF)


def fwd_dft_kernel(s_ref, tab_ref, *refs):
    pieces, (out, scr, rc) = refs[:8], refs[-3:]
    r = s_ref[2]
    rows = pieces[0].shape[1]
    cols = pieces[0].shape[2]
    nms, nb = out.shape[0], out.shape[1]

    def body(c2, carry):
        for u in range(2):
            c = c2 * 2 + u
            for t in range(8):
                row = pl.multiple_of(((t & 3) ^ r) * rows, rows)
                q = t >> 2
                rc[u, pl.ds(row, rows), q * cols:(q + 1) * cols] = pieces[t][c]
        for u in range(2):
            c = c2 * 2 + u
            res = lax.dot_general(tab_ref[0], rc[u], NT, preferred_element_type=F32)
            for j in range(res.shape[1] // 128):
                scr[j, pl.ds(c, nms, stride=nb + 1), :] = res[:, j * 128:(j + 1) * 128]
        return carry

    lax.fori_loop(0, nb // 2, body, 0)

    def flush(i, carry):
        for j in range(scr.shape[0]):
            for u in range(32):
                out[i * 32 + u, :, j * 128:(j + 1) * 128] = scr[j, pl.ds((i * 32 + u) * (nb + 1), nb), :].astype(BF)
        return carry

    lax.fori_loop(0, nms // 32, flush, 0)


def fwd_leg_kernel(nf, s_ref, *refs):
    pws, fs = refs[:NV], refs[NV:NV + nf]
    mine, send = refs[-2 * NV:-NV], refs[-NV:]
    h = s_ref[3]
    gran = pl.program_id(0) // (MG // MB)
    nl = pws[0].shape[2]
    for g in range(NV):
        @pl.when(gran == g)
        def _(g=g):
            def body(m8, carry):
                for u in range(8):
                    m = m8 * 8 + u
                    x = jnp.concatenate([f[2 * m + s] for s in range(2) for f in fs], axis=0)
                    p = jnp.concatenate([pws[v][m, h] for v in range(g, NV)] + [pws[v][m, 1 - h] for v in range(g, NV)], axis=0)
                    res = lax.dot_general(p, x, NT, preferred_element_type=F32).astype(BF)
                    for v in range(g, NV):
                        for b in range(nl // LB):
                            at = (v - g) * nl + b * LB
                            mine[v][b, m] = res[at:at + LB]
                            at += (NV - g) * nl
                            send[v][b, m] = res[at:at + LB]
                return carry

            lax.fori_loop(0, MB // 8, body, 0)


def mix_kernel(vs, s_ref, wre, wim, *refs):
    ins = {v: refs[4 * n:4 * n + 4] for n, v in enumerate(vs)}
    outs = {v: refs[4 * len(vs) + 2 * n:4 * len(vs) + 2 * n + 2] for n, v in enumerate(vs)}
    scr_a, scr_b = refs[-2:]
    h = s_ref[3]
    for n, v in enumerate(vs):
        @pl.when(pl.program_id(0) // 2 == n)
        def _(v=v):
            nm = MG * (v + 1)

            def fill(i, carry):
                for u in range(16):
                    rows = pl.ds((i * 16 + u) * PAD, LB)
                    for half in range(2):
                        scr_a[2 * half + h, rows, :] = ins[v][half][0, i * 16 + u].astype(F32)
                        scr_a[2 * half + 1 - h, rows, :] = ins[v][2 + half][0, i * 16 + u].astype(F32)
                return carry

            lax.fori_loop(0, nm // 16, fill, 0)

            def body(li2, carry):
                for u in range(2):
                    li = li2 * 2 + u
                    lhs = jnp.concatenate([scr_a[b, pl.ds(li, nm, stride=PAD), :].astype(BF) for b in range(4)], axis=1)
                    wr, wi = wre[li], wim[li]
                    ni = -wi
                    cg = wr.shape[0] // 4
                    rhs = jnp.concatenate([jnp.concatenate([w[b * cg:(b + 1) * cg] for b in range(4) for w in pair], axis=0)
                                           for pair in ((wr, ni), (wi, wr))], axis=1)
                    res = jnp.dot(lhs, rhs, preferred_element_type=F32)
                    for b in range(2):
                        scr_b[b, pl.ds(li, nm, stride=PAD), :] = res[:, b * 128:(b + 1) * 128]
                return carry

            lax.fori_loop(0, LB // 2, body, 0)
            low = lax.broadcasted_iota(jnp.int32, (LB, 128), 1) < 64
            first_is_mine = h == 0

            def flush(i, carry):
                for u in range(16):
                    rows = pl.ds((i * 16 + u) * PAD, LB)
                    re, im = scr_b[0, rows, :], scr_b[1, rows, :]
                    zero = jnp.where(low, re, pltpu.roll(im, 64, 1))
                    one = jnp.where(low, pltpu.roll(re, 64, 1), im)
                    outs[v][0][0, i * 16 + u] = jnp.where(first_is_mine, zero, one).astype(BF)
                    outs[v][1][0, i * 16 + u] = jnp.where(first_is_mine, one, zero).astype(BF)
                return carry

            lax.fori_loop(0, nm // 16, flush, 0)


def inv_leg_kernel(offs, s_ref, *refs):
    pis, bm, br = refs[:NV], refs[NV:2 * NV], refs[2 * NV:3 * NV]
    outs = refs[-len(offs):]
    h = s_ref[3]
    gran = pl.program_id(0) // (MG // MB)
    for g in range(NV):
        @pl.when(gran == g)
        def _(g=g):
            def body(m8, carry):
                for u in range(8):
                    m = m8 * 8 + u
                    b = jnp.concatenate([x[v][lb, m] for x in (bm, br) for v in range(g, NV) for lb in range(2)], axis=0)
                    p = jnp.concatenate([pis[v][m, h] for v in range(g, NV)] + [pis[v][m, 1 - h] for v in range(g, NV)], axis=0)
                    y = lax.dot_general(b, p, TN, preferred_element_type=F32).astype(BF)
                    for o, off in zip(outs, offs):
                        n = o.shape[1]
                        for s in range(2):
                            o[2 * m + s] = y[s * 64 + off:s * 64 + off + n]
                return carry

            lax.fori_loop(0, MB // 8, body, 0)


def inv_dft_kernel(s_ref, tab_ref, g_ref, *refs):
    pieces, (scr, yc) = refs[-10:-2], refs[-2:]
    r = s_ref[2]
    rows = pieces[0].shape[1]
    cols = pieces[0].shape[2]
    nms, nb = g_ref.shape[0], g_ref.shape[1]

    def fill(i, carry):
        for j in range(scr.shape[0]):
            for u in range(32):
                scr[j, pl.ds((i * 32 + u) * (nb + 1), nb), :] = g_ref[i * 32 + u, :, j * 128:(j + 1) * 128].astype(F32)
        return carry

    lax.fori_loop(0, nms // 32, fill, 0)

    def body(c2, carry):
        for u in range(2):
            c = c2 * 2 + u
            g = jnp.concatenate([scr[j, pl.ds(c, nms, stride=nb + 1), :].astype(BF) for j in range(scr.shape[0])], axis=1)
            yc[u] = lax.dot_general(g, tab_ref[0], TN, preferred_element_type=F32).astype(BF)
        for u in range(2):
            c = c2 * 2 + u
            for t in range(8):
                row = pl.multiple_of(((t & 3) ^ r) * rows, rows)
                q = t >> 2
                pieces[t][c] = yc[u, pl.ds(row, rows), q * cols:(q + 1) * cols]
        return carry

    lax.fori_loop(0, nb // 2, body, 0)


def gelu(y):
    return 0.5 * y * (1.0 + lax.erf(y * math.sqrt(0.5)))


def final_kernel(s_ref, f_ref, *refs):
    pieces, (out, buf) = refs[:8], refs[-2:]
    t = pl.program_id(0)
    for n in range(8):
        @pl.when(t == n)
        def _(n=n):
            buf[...] = pieces[n][...]

    def body(c, carry):
        out[0, 0, 0, c] = f_ref[0, 0, 0, c] + gelu(buf[c].astype(F32))
        return carry

    lax.fori_loop(0, buf.shape[0], body, 0)


def call(kernel, grid, in_specs, out_specs, out_shape, flops, nbytes, scratch=(), deps=(), alias=None, vmem=32):
    fn = pl.pallas_call(
        kernel,
        grid_spec=pltpu.PrefetchScalarGridSpec(
            num_scalar_prefetch=1, grid=grid,
            in_specs=list(in_specs) + [pl.BlockSpec(memory_space=pl.ANY)] * len(deps),
            out_specs=out_specs, scratch_shapes=list(scratch)),
        out_shape=out_shape,
        input_output_aliases=alias or {},
        compiler_params=pltpu.CompilerParams(dimension_semantics=("arbitrary",) * len(grid), vmem_limit_bytes=vmem * 2 ** 20),
        cost_estimate=pl.CostEstimate(flops=int(flops), bytes_accessed=int(nbytes), transcendentals=0),
    )
    return lambda *args: fn(*args, *deps)


def solution(mesh):
    lat_devs = mesh.shape['lat']
    lon_devs = mesh.shape['lon']
    nd = lat_devs * lon_devs

    def local_layer(grid_field, mix_weight):
        batch, channels, row_count, col_count = grid_field.shape
        n_lat = row_count * lat_devs
        n_lon = col_count * lon_devs
        n_deg = mix_weight.shape[0]
        half_c = batch * channels // nd
        nms = 2 * n_deg
        lv = n_deg // 2 // NV
        q = lax.axis_index('lon')
        r = lax.axis_index('lat')
        me = q * lat_devs + r
        h = r % 2
        scal = jnp.stack([me, q, r, h]).astype(jnp.int32)
        pw_np, pi_np = legendre_tables(n_lat, n_lon, n_deg)
        tf_np, ti_np = dft_tables(n_lon, n_deg)
        pw, pi = [jnp.asarray(x) for x in pw_np], [jnp.asarray(x) for x in pi_np]
        tf, ti = jnp.asarray(tf_np), jnp.asarray(ti_np)
        f6 = grid_field.reshape(batch, 2, channels // half_c, half_c // 2, row_count, col_count)

        def swap(x, t):
            if t == 0:
                return x
            return lax.ppermute(x, ('lon', 'lat'), [(s, s ^ t) for s in range(nd)])

        def piece(cc):
            return jax.ShapeDtypeStruct((cc, row_count, col_count), BF)

        tab_spec = pl.BlockSpec((1, nms, n_lon), lambda i, s: (s[1], 0, 0))

        def piece_spec(nb):
            return pl.BlockSpec((nb, row_count, col_count), lambda i, s: (i, 0, 0))

        def dft_scratch(nb):
            return [pltpu.VMEM((n_lat // 128, nms * (nb + 1), 128), F32), pltpu.VMEM((2, n_lat, n_lon), BF)]

        def cast_chunk(half, c0, cc):
            cb = 8
            base = c0 // cb
            return call(
                cast_kernel, (cc // cb,),
                [pl.BlockSpec((1, 1, 1, cb, row_count, col_count),
                              functools.partial(lambda t, i, s: ((s[0] ^ t) // 2, half, (s[0] ^ t) % 2, base + i, 0, 0), t)) for t in range(nd)],
                [pl.BlockSpec((cb, row_count, col_count), lambda i, s: (i, 0, 0))] * nd,
                [piece(cc)] * nd, 1e6, nd * cc * row_count * col_count * 6, vmem=16)(scal, *([f6] * nd))

        def dft_chunk(pieces, cc, nb, deps):
            return call(
                fwd_dft_kernel, (cc // nb,),
                [tab_spec] + [piece_spec(nb)] * nd,
                pl.BlockSpec((nms, nb, n_lat), lambda i, s: (0, i, 0)),
                jax.ShapeDtypeStruct((nms, cc, n_lat), BF),
                4.0 * cc * nms * n_lat * n_lon, cc * nms * n_lat * 6, dft_scratch(nb), deps)(scal, tf, *pieces)

        last = [MG // MB * (v + 1) - 1 for v in range(NV)]
        tri_specs = [pl.BlockSpec((MB, 2, lv, n_lat), functools.partial(lambda v, i, s: (jnp.minimum(i, last[v]), 0, 0, 0), v)) for v in range(NV)]
        spec_specs = [pl.BlockSpec((lv // LB, MB, LB, half_c), functools.partial(lambda v, i, s: (0, jnp.minimum(i, last[v]), 0, 0), v)) for v in range(NV)]
        spec_shapes = [jax.ShapeDtypeStruct((lv // LB, MG * (v + 1), LB, half_c), BF) for v in range(NV)]

        def f_spec(cc):
            return pl.BlockSpec((2 * MB, cc, n_lat), lambda i, s: (i, 0, 0))

        def leg_fwd(fs):
            res = call(
                functools.partial(fwd_leg_kernel, len(fs)), (n_deg // MB,),
                tri_specs + [f_spec(f.shape[1]) for f in fs],
                spec_specs * 2, spec_shapes * 2,
                1.3 * n_deg * n_deg * n_lat * half_c, 50e6, vmem=26)(scal, *pw, *fs)
            return res[:NV], res[NV:]

        def leg_inv(offs, ccs, mine, recv):
            return call(
                functools.partial(inv_leg_kernel, offs), (n_deg // MB,),
                tri_specs + spec_specs * 2,
                [f_spec(cc) for cc in ccs],
                [jax.ShapeDtypeStruct((nms, cc, n_lat), BF) for cc in ccs],
                1.3 * n_deg * n_deg * n_lat * half_c, 50e6, vmem=26)(scal, *pi, *mine, *recv)

        sizes = HALVES[0] + HALVES[1]
        starts = [(half, sum(part[:k])) for half, part in enumerate(HALVES) for k in range(len(part))]
        recv = []
        for (half, c0), cc in zip(starts, sizes):
            k = len(recv)
            pieces = cast_chunk(half, c0, cc)
            recv.append([swap(p, t) for t, p in enumerate(pieces)])

        w = mix_weight.reshape(n_deg // (2 * LB), 2, LB, channels, channels, 2)
        w = lax.dynamic_index_in_dim(w, h, axis=1, keepdims=False).reshape(n_deg // 2, channels, channels, 2)
        oh = channels // 2
        w_parts = [[w[:, :, x * oh:(x + 1) * oh, p] for p in range(2)] for x in range(2)]

        a_mine, a_recv, prev = [], [], []
        k = 0
        for half in range(2):
            fs = []
            for cc in HALVES[half]:
                deps = list(prev)
                if k == 1:
                    deps += w_parts[0] + w_parts[1]
                elif k == len(HALVES[0]):
                    deps += [a_mine[0][0]]
                fs.append(dft_chunk(recv[k], cc, 8 if k == len(sizes) - 1 else 16, deps))
                prev = fs[-1:]
                k += 1
            mine, send = leg_fwd(fs)
            a_mine.append(mine)
            got = [None] * NV
            for v in sum(MIX, ()):
                got[v] = swap(send[v], 1)
            a_recv.append(got)

        def mix(vs, out_half):
            jump = [lambda j: jnp.minimum(j, 1), lambda j: jnp.maximum(j - 2, 0)]
            w_spec = pl.BlockSpec((LB, channels, channels // 2), lambda j, s: (jnp.where(j < 2, 2 * vs[0] + j, 2 * vs[-1] + j - 2), 0, 0))
            specs, outs, shapes, args = [], [], [], []
            for n, v in enumerate(vs):
                spec = pl.BlockSpec((1, MG * (v + 1), LB, half_c), functools.partial(lambda n, j, s: (jump[n](j), 0, 0, 0), n))
                specs += [spec] * 4
                outs += [spec] * 2
                shapes += [spec_shapes[v]] * 2
                args += [a_mine[0][v], a_mine[1][v], a_recv[0][v], a_recv[1][v]]
            rows = MG * (vs[0] + 1) * PAD
            return call(
                functools.partial(mix_kernel, vs), (2 * len(vs),), [w_spec, w_spec] + specs, outs, shapes,
                4.0 * 4 * LB * MG * (vs[0] + 1) * channels * channels, 40e6,
                [pltpu.VMEM((4, rows, 128), F32), pltpu.VMEM((2, rows, 128), F32)], vmem=40)(scal, *w_parts[out_half], *args)

        def mix_half(half):
            mine, recv = [None] * NV, [None] * NV
            for vs in MIX:
                res = mix(vs, half)
                for n, v in enumerate(vs):
                    mine[v] = res[2 * n]
                    recv[v] = swap(res[2 * n + 1], 1)
            return mine, recv

        def idft_chunk(g, nb):
            cc = g.shape[1]
            return call(
                inv_dft_kernel, (cc // nb,),
                [tab_spec, pl.BlockSpec((nms, nb, n_lat), lambda i, s: (0, i, 0))],
                [piece_spec(nb)] * nd, [piece(cc)] * nd,
                4.0 * cc * nms * n_lat * n_lon, cc * nms * n_lat * 6, dft_scratch(nb))(scal, ti, g)

        def final_chunk(half, c0, cc, pieces, out):
            cb = 8
            base, nb = c0 // cb, cc // cb
            big = pl.BlockSpec((1, 1, 1, cb, row_count, col_count), lambda t, i, s: ((s[0] ^ t) // 2, half, (s[0] ^ t) % 2, base + i, 0, 0))

            def own(n):
                return pl.BlockSpec((cb, row_count, col_count),
                                    lambda t, i, s: (jnp.where(t == n, i, jnp.where(t < n, 0, nb - 1)), 0, 0))

            deps = [] if out is None else [out]
            return call(
                final_kernel, (nd, nb), [big] + [own(n) for n in range(nd)], big,
                jax.ShapeDtypeStruct(f6.shape, F32), 40 * nd * cc * row_count * col_count, 10 * nd * cc * row_count * col_count,
                [pltpu.VMEM((cb, row_count, col_count), BF)], deps,
                {2 + nd: 0} if deps else None, 16)(scal, f6, *pieces)

        k = 0
        out = None
        for half in range(2):
            b_mine, b_recv = mix_half(half)
            offs = [c0 for hf, c0 in starts if hf == half]
            groups = [[0], list(range(1, len(offs)))] if half == 0 else [list(range(len(offs)))]
            gs = []
            for group in groups:
                gs += leg_inv([offs[x] for x in group], [HALVES[half][x] for x in group], b_mine, b_recv)
            for g in gs:
                cc = g.shape[1]
                pieces = idft_chunk(g, 8 if k == 0 else 16)
                got = [swap(p, t) for t, p in enumerate(pieces)]
                if k < len(sizes) - 1:
                    out = final_chunk(*starts[k], cc, got, out)
                else:
                    for t, p in enumerate(got):
                        at = ((me ^ t) // 2, starts[k][0], (me ^ t) % 2, starts[k][1], 0, 0)
                        src = lax.dynamic_slice(f6, at, (1, 1, 1, cc, row_count, col_count))
                        out = lax.dynamic_update_slice(out, src + gelu(p.astype(F32))[None, None, None], at)
                k += 1
        return out.reshape(grid_field.shape)

    field_spec = P('member', None, 'lat', 'lon')
    return jax.shard_map(local_layer, mesh=mesh, in_specs=(field_spec, P()), out_specs=field_spec, check_vma=False)
```

profile of v0, /device:TPU:0, one launch (start us, length us, event | category | flops | bytes accessed | tf_op | source)
XLA Modules:
  0.0 1129.3 jit_solution(15732303057122124530)
XLA Ops:
  36.4 21.1 %collective-permute-done.4.refs_5_ = bf16[16,64,256]{2,1,0:T(8,128)(2,1)} collective-permute-done((bf16[16,64,256]{2,1,0:T(8,128)(2,1)}, bf16[16,64,256]{2,1,0:T(8,128)(2,1)}, u32[]{:S(2)}, u32[]{:S(2)}) %collective-permute-start.4) | collective-permute-done | bytes 524320 | tf_op jit(solution)/shard_map/ppermute | solution.py:297
  119.6 26.7 %constant_dynamic-slice_fusion = bf16[8,1,16,256,256,2]{4,5,3,2,1,0:T(2,128)(2,1)} fusion(bf16[8,2,16,256,256,2]{4,5,3,2,1,0:T(2,128)(2,1)} %bitcast.5, s32[]{:T(128)S(6)} %select_n.133), kind=kLoop, calls=%fused_computation.68 | loop fusion | bytes 67108864 | tf_op jit(solution)/shard_map/jit(dynamic_index_in_dim)/dynamic_slice | solution.py:361
  146.2 23.0 %copy.17 = bf16[8,1,16,256,256,2]{4,3,2,0,5,1:T(8,128)(2,1)} copy(bf16[8,1,16,256,256,2]{4,5,3,2,1,0:T(2,128)(2,1)} %constant_dynamic-slice_fusion) | data formatting | bytes 67108864
  169.2 18.0 %collective-permute-done.29.refs_2_ = bf16[16,64,256]{2,1,0:T(8,128)(2,1)} collective-permute-done((bf16[16,64,256]{2,1,0:T(8,128)(2,1)}, bf16[16,64,256]{2,1,0:T(8,128)(2,1)}, u32[]{:S(2)}, u32[]{:S(2)}) %collective-permute-start.29) | collective-permute-done | bytes 524320 | tf_op jit(solution)/shard_map/ppermute | solution.py:297
  191.9 23.0 %slice_bitcast_fusion = (bf16[128,256,128]{2,1,0:T(8,128)(2,1)}, bf16[128,256,128]{2,1,0:T(8,128)(2,1)}, bf16[128,256,128]{2,1,0:T(8,128)(2,1)}, bf16[128,256,128]{2,1,0:T(8,128)(2,1)}) fusion(bf16[128,256,256,2]{2,1,0,3:T(8,128)(2,1)} %bitcast.68), kind=kLoop, calls=%fused_computation | loop fusion | bytes 67108864 | tf_op jit(solution)/shard_map/squeeze | solution.py:363
  226.0 65.9 %collective-permute-done.10.refs_4_ = bf16[48,64,256]{2,1,0:T(8,128)(2,1)S(1)} collective-permute-done((bf16[48,64,256]{2,1,0:T(8,128)(2,1)}, bf16[48,64,256]{2,1,0:T(8,128)(2,1)S(1)}, u32[]{:S(2)}, u32[]{:S(2)}) %collective-permute-start.10) | collective-permute-done | bytes 1572896 | tf_op jit(solution)/shard_map/ppermute | solution.py:297
  295.4 30.2 %collective-permute-done.11.refs_5_ = bf16[48,64,256]{2,1,0:T(8,128)(2,1)S(1)} collective-permute-done((bf16[48,64,256]{2,1,0:T(8,128)(2,1)}, bf16[48,64,256]{2,1,0:T(8,128)(2,1)S(1)}, u32[]{:S(2)}, u32[]{:S(2)}) %collective-permute-start.11) | collective-permute-done | bytes 1572896 | tf_op jit(solution)/shard_map/ppermute | solution.py:297
  340.5 18.2 %shard_map.121.refs_5_.refs_8_ = bf16[512,48,256]{2,1,0:T(8,128)(2,1)} custom-call(s32[4]{0:T(128)S(1)} %pad_add_fusion.s_ref, bf16[2,512,512]{2,1,0:T(8,128)(2,1)S(1)} %copy-done.21, bf16[48,64,256]{2,1,0:T(8,128)(2,1)S(1)} %get-tuple-element.128.refs_0_, bf16[48,64,256]{2,1,0:T(8,128)(2,1)} %collective-permute-done.7.refs_1_, ...), custom_call_target="tpu_custom_call" | custom-call | flops 12884901888 | bytes 37748736 | tf_op jit(solution)/shard_map/pallas_call | solution.py:267
  360.4 17.3 %shard_map.122 = (bf16[2,64,16,128]{3,2,1,0:T(8,128)(2,1)S(1)}, bf16[2,128,16,128]{3,2,1,0:T(8,128)(2,1)S(1)}, bf16[2,192,16,128]{3,2,1,0:T(8,128)(2,1)S(1)}, bf...) custom-call(s32[4]{0:T(128)S(1)} %pad_add_fusion.s_ref, ...), custom_call_target="tpu_custom_call" | custom-call | flops 2791728640 | bytes 50000000 | tf_op jit(solution)/shard_map/pallas_call | solution.py:267
  380.5 13.1 %collective-permute-done.17.refs_4_ = bf16[32,64,256]{2,1,0:T(8,128)(2,1)} collective-permute-done((bf16[32,64,256]{2,1,0:T(8,128)(2,1)}, bf16[32,64,256]{2,1,0:T(8,128)(2,1)}, u32[]{:S(2)}, u32[]{:S(2)}) %collective-permute-start.17) | collective-permute-done | bytes 1048608 | tf_op jit(solution)/shard_map/ppermute | solution.py:297
  395.4 20.2 %collective-permute-done.18.refs_5_ = bf16[32,64,256]{2,1,0:T(8,128)(2,1)} collective-permute-done((bf16[32,64,256]{2,1,0:T(8,128)(2,1)}, bf16[32,64,256]{2,1,0:T(8,128)(2,1)}, u32[]{:S(2)}, u32[]{:S(2)}) %collective-permute-start.18) | collective-permute-done | bytes 1048608 | tf_op jit(solution)/shard_map/ppermute | solution.py:297
  419.2 13.1 %shard_map.124.refs_8_.refs_4_ = bf16[512,32,256]{2,1,0:T(8,128)(2,1)S(1)} custom-call(s32[4]{0:T(128)S(1)} %pad_add_fusion.s_ref, bf16[2,512,512]{2,1,0:T(8,128)(2,1)S(1)} %copy-done.22, bf16[32,64,256]{2,1,0:T(8,128)(2,1)S(1)} %copy-done.119, bf16[32,64,256]{2,1,0:T(8,128)(2,1)} %collective-permute-done.14.refs_1_, ...), custom_call_target="tpu_custom_call" | custom-call | flops 8589934592 | bytes 25165824 | tf_op jit(solution)/shard_map/pallas_call | solution.py:267
  476.1 16.9 %shard_map.129 = (bf16[2,64,16,128]{3,2,1,0:T(8,128)(2,1)S(1)}, bf16[2,128,16,128]{3,2,1,0:T(8,128)(2,1)S(1)}, bf16[2,192,16,128]{3,2,1,0:T(8,128)(2,1)S(1)}, bf...) custom-call(s32[4]{0:T(128)S(1)} %pad_add_fusion.s_ref, ...), custom_call_target="tpu_custom_call" | custom-call | flops 2791728640 | bytes 50000000 | tf_op jit(solution)/shard_map/pallas_call | solution.py:267
  504.8 14.0 %shard_map.130 = (bf16[2,128,16,128]{3,2,1,0:T(8,128)(2,1)S(1)}, bf16[2,128,16,128]{3,2,1,0:T(8,128)(2,1)}, bf16[2,64,16,128]{3,2,1,0:T(8,128)(2,1)S(1)}, bf16[2,64,16,128]{3,2,1,0:T(8,128)(2,1)S(1)}) custom-call(s32[4]{0:T(128)S(1)} %pad_add_fusion.s_ref, bf16[128,256,128]{2,1,0:T(8,128)(2,1)} %get-tuple-element.238.refs_11_.wre, ...), custom_call_target="tpu_custom_call" | custom-call | flops 2147483648 | bytes 40000000 | tf_op jit(solution)/shard_map/pallas_call | solution.py:267
  522.8 12.8 %shard_map.132 = (bf16[2,256,16,128]{3,2,1,0:T(8,128)(2,1)S(1)}, bf16[2,256,16,128]{3,2,1,0:T(8,128)(2,1)}) custom-call(s32[4]{0:T(128)S(1)} %pad_add_fusion.s_ref, bf16[128,256,128]{2,1,0:T(8,128)(2,1)} %get-tuple-element.238.refs_11_.wre, bf16[128,256,128]{2,1,0:T(8,128)(2,1)} %get-tuple-element.237.refs_12_.wim, bf16[2,256,16,128]{3,2,1,0:T(8,128)(2,1)S(1)} %copy-done.16, ...), custom_call_target="tpu_custom_call" | custom-call | flops 4294967296 | bytes 40000000 | tf_op jit(solution)/shard_map/pallas_call | solution.py:267
  546.7 12.8 %shard_map.138 = (bf16[2,256,16,128]{3,2,1,0:T(8,128)(2,1)S(1)}, bf16[2,256,16,128]{3,2,1,0:T(8,128)(2,1)}) custom-call(s32[4]{0:T(128)S(1)} %pad_add_fusion.s_ref, bf16[128,256,128]{2,1,0:T(8,128)(2,1)} %get-tuple-element.236.refs_9_.wre, bf16[128,256,128]{2,1,0:T(8,128)(2,1)} %get-tuple-element.235.refs_10_.wim, bf16[2,256,16,128]{3,2,1,0:T(8,128)(2,1)S(1)} %copy-done.16, ...), custom_call_target="tpu_custom_call" | custom-call | flops 4294967296 | bytes 40000000 | tf_op jit(solution)/shard_map/pallas_call | solution.py:267
  573.3 14.3 %shard_map.136 = (bf16[2,128,16,128]{3,2,1,0:T(8,128)(2,1)S(1)}, bf16[2,128,16,128]{3,2,1,0:T(8,128)(2,1)}, bf16[2,64,16,128]{3,2,1,0:T(8,128)(2,1)S(1)}, bf16[2,64,16,128]{3,2,1,0:T(8,128)(2,1)S(1)}) custom-call(s32[4]{0:T(128)S(1)} %pad_add_fusion.s_ref, bf16[128,256,128]{2,1,0:T(8,128)(2,1)} %get-tuple-element.236.refs_9_.wre, ...), custom_call_target="tpu_custom_call" | custom-call | flops 2147483648 | bytes 40000000 | tf_op jit(solution)/shard_map/pallas_call | solution.py:267
  593.4 16.4 %shard_map.133 = (bf16[512,32,256]{2,1,0:T(8,128)(2,1)}, bf16[512,16,256]{2,1,0:T(8,128)(2,1)S(1)}, bf16[512,16,256]{2,1,0:T(8,128)(2,1)S(1)}) custom-call(s32[4]{0:T(128)S(1)} %pad_add_fusion.s_ref, bf16[64,2,32,256]{3,2,1,0:T(8,128)(2,1)S(1)} %copy-done.2, bf16[128,2,32,256]{3,2,1,0:T(8,128)(2,1)S(1)} %copy-done, ...), custom_call_target="tpu_custom_call" | custom-call | flops 2791728640 | bytes 50000000 | tf_op jit(solution)/shard_map/pallas_call | solution.py:267
  622.8 14.0 %shard_map.141.g_ref = bf16[512,16,256]{2,1,0:T(8,128)(2,1)S(1)} custom-call(s32[4]{0:T(128)S(1)} %pad_add_fusion.s_ref, bf16[64,2,32,256]{3,2,1,0:T(8,128)(2,1)S(1)} %copy-done.3, bf16[128,2,32,256]{3,2,1,0:T(8,128)(2,1)S(1)} %copy-done, bf16[192,2,32,256]{3,2,1,0:T(8,128)(2,1)S(1)} %bitcast.65, bf16[256,2,32,256]{3,2,1,0:T(8,128)(2,1)} %constant.165.clone.refs_3_, ...), custom_call_target="tpu_custom_call" | custom-call | flops 2791728640 | bytes 50000000 | tf_op jit(solution)/shard_map/pallas_call | solution.py:267
  674.7 16.9 %shard_map.139.g_ref = bf16[512,48,256]{2,1,0:T(8,128)(2,1)} custom-call(s32[4]{0:T(128)S(1)} %pad_add_fusion.s_ref, bf16[64,2,32,256]{3,2,1,0:T(8,128)(2,1)S(1)} %copy-done.4, bf16[128,2,32,256]{3,2,1,0:T(8,128)(2,1)S(1)} %copy-done, bf16[192,2,32,256]{3,2,1,0:T(8,128)(2,1)S(1)} %bitcast.65, bf16[256,2,32,256]{3,2,1,0:T(8,128)(2,1)} %constant.165.clone.refs_3_, ...), custom_call_target="tpu_custom_call" | custom-call | flops 2791728640 | bytes 50000000 | tf_op jit(solution)/shard_map/pallas_call | solution.py:267
  695.6 17.4 %shard_map.140 = (bf16[48,64,256]{2,1,0:T(8,128)(2,1)S(1)}, bf16[48,64,256]{2,1,0:T(8,128)(2,1)S(1)}, bf16[48,64,256]{2,1,0:T(8,128)(2,1)S(1)}, bf16[48,64,256]{...) custom-call(s32[4]{0:T(128)S(1)} %pad_add_fusion.s_ref, ...), custom_call_target="tpu_custom_call" | custom-call | flops 12884901888 | bytes 37748736 | tf_op jit(solution)/shard_map/pallas_call | solution.py:267
  713.0 37.9 %collective-permute-done.78.refs_7_ = bf16[16,64,256]{2,1,0:T(8,128)(2,1)S(1)} collective-permute-done((bf16[16,64,256]{2,1,0:T(8,128)(2,1)S(1)}, bf16[16,64,256]{2,1,0:T(8,128)(2,1)S(1)}, u32[]{:S(2)}, u32[]{:S(2)}) %collective-permute-start.78) | collective-permute-done | bytes 524320 | tf_op jit(solution)/shard_map/ppermute | solution.py:297
  760.2 19.9 %collective-permute-done.58.refs_5_ = bf16[32,64,256]{2,1,0:T(8,128)(2,1)S(1)} collective-permute-done((bf16[32,64,256]{2,1,0:T(8,128)(2,1)S(1)}, bf16[32,64,256]{2,1,0:T(8,128)(2,1)S(1)}, u32[]{:S(2)}, u32[]{:S(2)}) %collective-permute-start.58) | collective-permute-done | bytes 1048608 | tf_op jit(solution)/shard_map/ppermute | solution.py:297
  782.2 31.0 %collective-permute-done.59.refs_6_ = bf16[32,64,256]{2,1,0:T(8,128)(2,1)S(1)} collective-permute-done((bf16[32,64,256]{2,1,0:T(8,128)(2,1)S(1)}, bf16[32,64,256]{2,1,0:T(8,128)(2,1)S(1)}, u32[]{:S(2)}, u32[]{:S(2)}) %collective-permute-start.59) | collective-permute-done | bytes 1048608 | tf_op jit(solution)/shard_map/ppermute | solution.py:297
  815.2 19.1 %collective-permute-done.60.refs_7_ = bf16[32,64,256]{2,1,0:T(8,128)(2,1)S(1)} collective-permute-done((bf16[32,64,256]{2,1,0:T(8,128)(2,1)S(1)}, bf16[32,64,256]{2,1,0:T(8,128)(2,1)S(1)}, u32[]{:S(2)}, u32[]{:S(2)}) %collective-permute-start.60) | collective-permute-done | bytes 1048608 | tf_op jit(solution)/shard_map/ppermute | solution.py:297
  840.0 27.4 %collective-permute-done.67.refs_3_ = bf16[48,64,256]{2,1,0:T(8,128)(2,1)S(1)} collective-permute-done((bf16[48,64,256]{2,1,0:T(8,128)(2,1)S(1)}, bf16[48,64,256]{2,1,0:T(8,128)(2,1)S(1)}, u32[]{:S(2)}, u32[]{:S(2)}) %collective-permute-start.67) | collective-permute-done | bytes 1572896 | tf_op jit(solution)/shard_map/ppermute | solution.py:297
  872.8 96.9 %collective-permute-done.69.refs_5_ = bf16[48,64,256]{2,1,0:T(8,128)(2,1)S(1)} collective-permute-done((bf16[48,64,256]{2,1,0:T(8,128)(2,1)S(1)}, bf16[48,64,256]{2,1,0:T(8,128)(2,1)S(1)}, u32[]{:S(2)}, u32[]{:S(2)}) %collective-permute-start.69) | collective-permute-done | bytes 1572896 | tf_op jit(solution)/shard_map/ppermute | solution.py:297
  991.1 15.8 %shard_map.143.refs_8_ = f32[4,2,2,64,64,256]{5,4,3,2,1,0:T(8,128)} custom-call(s32[4]{0:T(128)S(1)} %pad_add_fusion.s_ref, f32[4,2,2,64,64,256]{5,4,3,2,1,0:T(8,128)} %bitcast.4.refs_0_.refs_1_.refs_2_.refs_3_.refs_4_.refs_5_.refs_6_.refs_7_.f_ref, bf16[16,64,256]{2,1,0:T(8,128)(2,1)S(1)} %copy-done.98, bf16[16,64,256]{2,1,0:T(8,128)(2,1)S(1)} %copy-done.100, ...), custom_call_target="tpu_custom_call" | custom-call | flops 83886080 | bytes 20971520 | tf_op jit(solution)/shard_map/pallas_call | solution.py:267
  1007.1 39.0 %shard_map.144.refs_8_ = f32[4,2,2,64,64,256]{5,4,3,2,1,0:T(8,128)} custom-call(s32[4]{0:T(128)S(1)} %pad_add_fusion.s_ref, f32[4,2,2,64,64,256]{5,4,3,2,1,0:T(8,128)} %bitcast.4.refs_0_.refs_1_.refs_2_.refs_3_.refs_4_.refs_5_.refs_6_.refs_7_.f_ref, bf16[48,64,256]{2,1,0:T(8,128)(2,1)S(1)} %get-tuple-element.210.refs_0_, ...), custom_call_target="tpu_custom_call", output_to_operand_aliasing={{}: (10, {})} | custom-call | flops 251658240 | bytes 62914560 | tf_op jit(solution)/shard_map/pallas_call | solution.py:267
  1046.2 26.3 %shard_map.145.refs_8_ = f32[4,2,2,64,64,256]{5,4,3,2,1,0:T(8,128)} custom-call(s32[4]{0:T(128)S(1)} %pad_add_fusion.s_ref, f32[4,2,2,64,64,256]{5,4,3,2,1,0:T(8,128)} %bitcast.4.refs_0_.refs_1_.refs_2_.refs_3_.refs_4_.refs_5_.refs_6_.refs_7_.f_ref, bf16[32,64,256]{2,1,0:T(8,128)(2,1)S(1)} %copy-done.72, ...), custom_call_target="tpu_custom_call", output_to_operand_aliasing={{}: (10, {})} | custom-call | flops 167772160 | bytes 41943040 | tf_op jit(solution)/shard_map/pallas_call | solution.py:267
  1076.0 14.4 %shard_map.146 = f32[4,2,2,64,64,256]{5,4,3,2,1,0:T(8,128)} custom-call(s32[4]{0:T(128)S(1)} %pad_add_fusion.s_ref, f32[4,2,2,64,64,256]{5,4,3,2,1,0:T(8,128)} %bitcast.4.refs_0_.refs_1_.refs_2_.refs_3_.refs_4_.refs_5_.refs_6_.refs_7_.f_ref, bf16[16,64,256]{2,1,0:T(8,128)(2,1)S(1)} %copy-done.90, ...), custom_call_target="tpu_custom_call", output_to_operand_aliasing={{}: (10, {})} | custom-call | flops 83886080 | bytes 20971520 | tf_op jit(solution)/shard_map/pallas_call | solution.py:267
  1105.2 16.8 %collective-permute-done.83 = bf16[16,64,256]{2,1,0:T(8,128)(2,1)S(1)} collective-permute-done((bf16[16,64,256]{2,1,0:T(8,128)(2,1)S(1)}, bf16[16,64,256]{2,1,0:T(8,128)(2,1)S(1)}, u32[]{:S(2)}, u32[]{:S(2)}) %collective-permute-start.83) | collective-permute-done | bytes 524320 | tf_op jit(solution)/shard_map/ppermute | solution.py:297
  (506 shorter events, 358.8 us)
Async XLA Ops:
  107.3 82.3 %collective-permute-start.7 = (bf16[48,64,256]{2,1,0:T(8,128)(2,1)}, bf16[48,64,256]{2,1,0:T(8,128)(2,1)}, u32[]{:S(2)}, u32[]{:S(2)}) collective-permute-start(bf16[48,64,256]{2,1,0:T(8,128)(2,1)} %get-tuple-element.129), channel_id=1, source_target_pairs={{0,1},{1,0},{2,3},{3,2},{4,5},{5,4},{6,7},{7,6}} | collective-permute-start | bytes 4718600 | tf_op jit(solution)/shard_map/ppermute | solution.py:297
  116.3 75.3 %collective-permute-start.8 = (bf16[48,64,256]{2,1,0:T(8,128)(2,1)}, bf16[48,64,256]{2,1,0:T(8,128)(2,1)}, u32[]{:S(2)}, u32[]{:S(2)}) collective-permute-start(bf16[48,64,256]{2,1,0:T(8,128)(2,1)} %get-tuple-element.130), channel_id=1, source_target_pairs={{0,2},{1,3},{2,0},{3,1},{4,6},{5,7},{6,4},{7,5}} | collective-permute-start | bytes 4718600 | tf_op jit(solution)/shard_map/ppermute | solution.py:297
  117.2 70.4 %collective-permute-start.14 = (bf16[32,64,256]{2,1,0:T(8,128)(2,1)}, bf16[32,64,256]{2,1,0:T(8,128)(2,1)}, u32[]{:S(2)}, u32[]{:S(2)}) collective-permute-start(bf16[32,64,256]{2,1,0:T(8,128)(2,1)} %get-tuple-element.138), channel_id=1, source_target_pairs={{0,1},{1,0},{2,3},{3,2},{4,5},{5,4},{6,7},{7,6}} | collective-permute-start | bytes 3145736 | tf_op jit(solution)/shard_map/ppermute | solution.py:297
  117.5 71.8 %collective-permute-start.15 = (bf16[32,64,256]{2,1,0:T(8,128)(2,1)}, bf16[32,64,256]{2,1,0:T(8,128)(2,1)}, u32[]{:S(2)}, u32[]{:S(2)}) collective-permute-start(bf16[32,64,256]{2,1,0:T(8,128)(2,1)} %get-tuple-element.139), channel_id=1, source_target_pairs={{0,2},{1,3},{2,0},{3,1},{4,6},{5,7},{6,4},{7,5}} | collective-permute-start | bytes 3145736 | tf_op jit(solution)/shard_map/ppermute | solution.py:297
  118.6 68.6 %collective-permute-start.29 = (bf16[16,64,256]{2,1,0:T(8,128)(2,1)}, bf16[16,64,256]{2,1,0:T(8,128)(2,1)}, u32[]{:S(2)}, u32[]{:S(2)}) collective-permute-start(bf16[16,64,256]{2,1,0:T(8,128)(2,1)} %get-tuple-element.156), channel_id=1, source_target_pairs={{0,2},{1,3},{2,0},{3,1},{4,6},{5,7},{6,4},{7,5}} | collective-permute-start | bytes 1572872 | tf_op jit(solution)/shard_map/ppermute | solution.py:297
  187.5 104.3 %collective-permute-start.10 = (bf16[48,64,256]{2,1,0:T(8,128)(2,1)}, bf16[48,64,256]{2,1,0:T(8,128)(2,1)S(1)}, u32[]{:S(2)}, u32[]{:S(2)}) collective-permute-start(bf16[48,64,256]{2,1,0:T(8,128)(2,1)} %copy-done.116), channel_id=1, source_target_pairs={{0,4},{1,5},{2,6},{3,7},{4,0},{5,1},{6,2},{7,3}} | collective-permute-start | bytes 4718600 | tf_op jit(solution)/shard_map/ppermute | solution.py:297
  189.3 136.3 %collective-permute-start.11 = (bf16[48,64,256]{2,1,0:T(8,128)(2,1)}, bf16[48,64,256]{2,1,0:T(8,128)(2,1)S(1)}, u32[]{:S(2)}, u32[]{:S(2)}) collective-permute-start(bf16[48,64,256]{2,1,0:T(8,128)(2,1)} %copy-done.115), channel_id=1, source_target_pairs={{0,5},{1,4},{2,7},{3,6},{4,1},{5,0},{6,3},{7,2}} | collective-permute-start | bytes 4718600 | tf_op jit(solution)/shard_map/ppermute | solution.py:297
  189.6 138.9 %collective-permute-start.12 = (bf16[48,64,256]{2,1,0:T(8,128)(2,1)}, bf16[48,64,256]{2,1,0:T(8,128)(2,1)S(1)}, u32[]{:S(2)}, u32[]{:S(2)}) collective-permute-start(bf16[48,64,256]{2,1,0:T(8,128)(2,1)} %copy-done.114), channel_id=1, source_target_pairs={{0,6},{1,7},{2,4},{3,5},{4,2},{5,3},{6,0},{7,1}} | collective-permute-start | bytes 4718600 | tf_op jit(solution)/shard_map/ppermute | solution.py:297
  191.6 138.7 %collective-permute-start.13 = (bf16[48,64,256]{2,1,0:T(8,128)(2,1)S(1)}, bf16[48,64,256]{2,1,0:T(8,128)(2,1)S(1)}, u32[]{:S(2)}, u32[]{:S(2)}) collective-permute-start(bf16[48,64,256]{2,1,0:T(8,128)(2,1)S(1)} %get-tuple-element.135), channel_id=1, source_target_pairs={{0,7},{1,6},{2,5},{3,4},{4,3},{5,2},{6,1},{7,0}} | collective-permute-start | bytes 4718600 | tf_op jit(solution)/shard_map/ppermute | solution.py:297
  224.5 154.1 %collective-permute-start.16 = (bf16[32,64,256]{2,1,0:T(8,128)(2,1)}, bf16[32,64,256]{2,1,0:T(8,128)(2,1)}, u32[]{:S(2)}, u32[]{:S(2)}) collective-permute-start(bf16[32,64,256]{2,1,0:T(8,128)(2,1)} %get-tuple-element.140), channel_id=1, source_target_pairs={{0,3},{1,2},{2,1},{3,0},{4,7},{5,6},{6,5},{7,4}} | collective-permute-start | bytes 3145736 | tf_op jit(solution)/shard_map/ppermute | solution.py:297
  293.0 100.6 %collective-permute-start.17 = (bf16[32,64,256]{2,1,0:T(8,128)(2,1)}, bf16[32,64,256]{2,1,0:T(8,128)(2,1)}, u32[]{:S(2)}, u32[]{:S(2)}) collective-permute-start(bf16[32,64,256]{2,1,0:T(8,128)(2,1)} %get-tuple-element.141), channel_id=1, source_target_pairs={{0,4},{1,5},{2,6},{3,7},{4,0},{5,1},{6,2},{7,3}} | collective-permute-start | bytes 3145736 | tf_op jit(solution)/shard_map/ppermute | solution.py:297
  326.8 88.8 %collective-permute-start.18 = (bf16[32,64,256]{2,1,0:T(8,128)(2,1)}, bf16[32,64,256]{2,1,0:T(8,128)(2,1)}, u32[]{:S(2)}, u32[]{:S(2)}) collective-permute-start(bf16[32,64,256]{2,1,0:T(8,128)(2,1)} %get-tuple-element.142), channel_id=1, source_target_pairs={{0,5},{1,4},{2,7},{3,6},{4,1},{5,0},{6,3},{7,2}} | collective-permute-start | bytes 3145736 | tf_op jit(solution)/shard_map/ppermute | solution.py:297
  329.7 87.7 %collective-permute-start.19 = (bf16[32,64,256]{2,1,0:T(8,128)(2,1)}, bf16[32,64,256]{2,1,0:T(8,128)(2,1)}, u32[]{:S(2)}, u32[]{:S(2)}) collective-permute-start(bf16[32,64,256]{2,1,0:T(8,128)(2,1)} %get-tuple-element.143), channel_id=1, source_target_pairs={{0,6},{1,7},{2,4},{3,5},{4,2},{5,3},{6,0},{7,1}} | collective-permute-start | bytes 3145736 | tf_op jit(solution)/shard_map/ppermute | solution.py:297
  331.5 86.5 %collective-permute-start.20 = (bf16[32,64,256]{2,1,0:T(8,128)(2,1)}, bf16[32,64,256]{2,1,0:T(8,128)(2,1)S(1)}, u32[]{:S(2)}, u32[]{:S(2)}) collective-permute-start(bf16[32,64,256]{2,1,0:T(8,128)(2,1)} %get-tuple-element.144), channel_id=1, source_target_pairs={{0,7},{1,6},{2,5},{3,4},{4,3},{5,2},{6,1},{7,0}} | collective-permute-start | bytes 3145736 | tf_op jit(solution)/shard_map/ppermute | solution.py:297
  378.5 63.7 %collective-permute-start.30 = (bf16[16,64,256]{2,1,0:T(8,128)(2,1)S(1)}, bf16[16,64,256]{2,1,0:T(8,128)(2,1)}, u32[]{:S(2)}, u32[]{:S(2)}) collective-permute-start(bf16[16,64,256]{2,1,0:T(8,128)(2,1)S(1)} %copy-done.147), channel_id=1, source_target_pairs={{0,3},{1,2},{2,1},{3,0},{4,7},{5,6},{6,5},{7,4}} | collective-permute-start | bytes 1572872 | tf_op jit(solution)/shard_map/ppermute | solution.py:297
  449.8 72.6 %collective-permute-start.41 = (bf16[2,256,16,128]{3,2,1,0:T(8,128)(2,1)}, bf16[2,256,16,128]{3,2,1,0:T(8,128)(2,1)S(1)}, u32[]{:S(2)}, u32[]{:S(2)}) collective-permute-start(bf16[2,256,16,128]{3,2,1,0:T(8,128)(2,1)} %get-tuple-element.177), channel_id=1, source_target_pairs={{0,1},{1,0},{2,3},{3,2},{4,5},{5,4},{6,7},{7,6}} | collective-permute-start | bytes 6291464 | tf_op jit(solution)/shard_map/ppermute | solution.py:297
  522.4 67.0 %collective-permute-start.44 = (bf16[2,128,16,128]{3,2,1,0:T(8,128)(2,1)}, bf16[2,128,16,128]{3,2,1,0:T(8,128)(2,1)}, u32[]{:S(2)}, u32[]{:S(2)}) collective-permute-start(bf16[2,128,16,128]{3,2,1,0:T(8,128)(2,1)} %get-tuple-element.181), channel_id=1, source_target_pairs={{0,1},{1,0},{2,3},{3,2},{4,5},{5,4},{6,7},{7,6}} | collective-permute-start | bytes 3145736 | tf_op jit(solution)/shard_map/ppermute | solution.py:297
  691.7 62.1 %collective-permute-start.55 = (bf16[32,64,256]{2,1,0:T(8,128)(2,1)S(1)}, bf16[32,64,256]{2,1,0:T(8,128)(2,1)S(1)}, u32[]{:S(2)}, u32[]{:S(2)}) collective-permute-start(bf16[32,64,256]{2,1,0:T(8,128)(2,1)S(1)} %get-tuple-element.196), channel_id=1, source_target_pairs={{0,2},{1,3},{2,0},{3,1},{4,6},{5,7},{6,4},{7,5}} | collective-permute-start | bytes 3145736 | tf_op jit(solution)/shard_map/ppermute | solution.py:297
  692.6 62.8 %collective-permute-start.56 = (bf16[32,64,256]{2,1,0:T(8,128)(2,1)S(1)}, bf16[32,64,256]{2,1,0:T(8,128)(2,1)S(1)}, u32[]{:S(2)}, u32[]{:S(2)}) collective-permute-start(bf16[32,64,256]{2,1,0:T(8,128)(2,1)S(1)} %get-tuple-element.197), channel_id=1, source_target_pairs={{0,3},{1,2},{2,1},{3,0},{4,7},{5,6},{6,5},{7,4}} | collective-permute-start | bytes 3145736 | tf_op jit(solution)/shard_map/ppermute | solution.py:297
  693.5 64.4 %collective-permute-start.57 = (bf16[32,64,256]{2,1,0:T(8,128)(2,1)S(1)}, bf16[32,64,256]{2,1,0:T(8,128)(2,1)S(1)}, u32[]{:S(2)}, u32[]{:S(2)}) collective-permute-start(bf16[32,64,256]{2,1,0:T(8,128)(2,1)S(1)} %get-tuple-element.198), channel_id=1, source_target_pairs={{0,4},{1,5},{2,6},{3,7},{4,0},{5,1},{6,2},{7,3}} | collective-permute-start | bytes 3145736 | tf_op jit(solution)/shard_map/ppermute | solution.py:297
  751.6 85.5 %collective-permute-start.65 = (bf16[48,64,256]{2,1,0:T(8,128)(2,1)S(1)}, bf16[48,64,256]{2,1,0:T(8,128)(2,1)S(1)}, u32[]{:S(2)}, u32[]{:S(2)}) collective-permute-start(bf16[48,64,256]{2,1,0:T(8,128)(2,1)S(1)} %get-tuple-element.211), channel_id=1, source_target_pairs={{0,1},{1,0},{2,3},{3,2},{4,5},{5,4},{6,7},{7,6}} | collective-permute-start | bytes 4718600 | tf_op jit(solution)/shard_map/ppermute | solution.py:297
  753.0 85.5 %collective-permute-start.66 = (bf16[48,64,256]{2,1,0:T(8,128)(2,1)S(1)}, bf16[48,64,256]{2,1,0:T(8,128)(2,1)S(1)}, u32[]{:S(2)}, u32[]{:S(2)}) collective-permute-start(bf16[48,64,256]{2,1,0:T(8,128)(2,1)S(1)} %get-tuple-element.212), channel_id=1, source_target_pairs={{0,2},{1,3},{2,0},{3,1},{4,6},{5,7},{6,4},{7,5}} | collective-permute-start | bytes 4718600 | tf_op jit(solution)/shard_map/ppermute | solution.py:297
  758.9 75.3 %collective-permute-start.60 = (bf16[32,64,256]{2,1,0:T(8,128)(2,1)S(1)}, bf16[32,64,256]{2,1,0:T(8,128)(2,1)S(1)}, u32[]{:S(2)}, u32[]{:S(2)}) collective-permute-start(bf16[32,64,256]{2,1,0:T(8,128)(2,1)S(1)} %copy-done.121), channel_id=1, source_target_pairs={{0,7},{1,6},{2,5},{3,4},{4,3},{5,2},{6,1},{7,0}} | collective-permute-start | bytes 3145736 | tf_op jit(solution)/shard_map/ppermute | solution.py:297
  781.2 86.2 %collective-permute-start.67 = (bf16[48,64,256]{2,1,0:T(8,128)(2,1)S(1)}, bf16[48,64,256]{2,1,0:T(8,128)(2,1)S(1)}, u32[]{:S(2)}, u32[]{:S(2)}) collective-permute-start(bf16[48,64,256]{2,1,0:T(8,128)(2,1)S(1)} %get-tuple-element.213), channel_id=1, source_target_pairs={{0,3},{1,2},{2,1},{3,0},{4,7},{5,6},{6,5},{7,4}} | collective-permute-start | bytes 4718600 | tf_op jit(solution)/shard_map/ppermute | solution.py:297
  835.2 134.4 %collective-permute-start.69 = (bf16[48,64,256]{2,1,0:T(8,128)(2,1)S(1)}, bf16[48,64,256]{2,1,0:T(8,128)(2,1)S(1)}, u32[]{:S(2)}, u32[]{:S(2)}) collective-permute-start(bf16[48,64,256]{2,1,0:T(8,128)(2,1)S(1)} %get-tuple-element.215), channel_id=1, source_target_pairs={{0,5},{1,4},{2,7},{3,6},{4,1},{5,0},{6,3},{7,2}} | collective-permute-start | bytes 4718600 | tf_op jit(solution)/shard_map/ppermute | solution.py:297
  837.1 134.9 %collective-permute-start.70 = (bf16[48,64,256]{2,1,0:T(8,128)(2,1)S(1)}, bf16[48,64,256]{2,1,0:T(8,128)(2,1)S(1)}, u32[]{:S(2)}, u32[]{:S(2)}) collective-permute-start(bf16[48,64,256]{2,1,0:T(8,128)(2,1)S(1)} %get-tuple-element.216), channel_id=1, source_target_pairs={{0,6},{1,7},{2,4},{3,5},{4,2},{5,3},{6,0},{7,1}} | collective-permute-start | bytes 4718600 | tf_op jit(solution)/shard_map/ppermute | solution.py:297
  839.7 146.4 %collective-permute-start.71 = (bf16[48,64,256]{2,1,0:T(8,128)(2,1)S(1)}, bf16[48,64,256]{2,1,0:T(8,128)(2,1)S(1)}, u32[]{:S(2)}, u32[]{:S(2)}) collective-permute-start(bf16[48,64,256]{2,1,0:T(8,128)(2,1)S(1)} %get-tuple-element.217), channel_id=1, source_target_pairs={{0,7},{1,6},{2,5},{3,4},{4,3},{5,2},{6,1},{7,0}} | collective-permute-start | bytes 4718600 | tf_op jit(solution)/shard_map/ppermute | solution.py:297
  868.5 204.0 %collective-permute-start.50 = (bf16[16,64,256]{2,1,0:T(8,128)(2,1)}, bf16[16,64,256]{2,1,0:T(8,128)(2,1)}, u32[]{:S(2)}, u32[]{:S(2)}) collective-permute-start(bf16[16,64,256]{2,1,0:T(8,128)(2,1)} %get-tuple-element.189), channel_id=1, source_target_pairs={{0,4},{1,5},{2,6},{3,7},{4,0},{5,1},{6,2},{7,3}} | collective-permute-start | bytes 1572872 | tf_op jit(solution)/shard_map/ppermute | solution.py:297
  870.8 202.5 %collective-permute-start.51 = (bf16[16,64,256]{2,1,0:T(8,128)(2,1)}, bf16[16,64,256]{2,1,0:T(8,128)(2,1)}, u32[]{:S(2)}, u32[]{:S(2)}) collective-permute-start(bf16[16,64,256]{2,1,0:T(8,128)(2,1)} %get-tuple-element.190), channel_id=1, source_target_pairs={{0,5},{1,4},{2,7},{3,6},{4,1},{5,0},{6,3},{7,2}} | collective-permute-start | bytes 1572872 | tf_op jit(solution)/shard_map/ppermute | solution.py:297
  970.8 103.1 %collective-permute-start.52 = (bf16[16,64,256]{2,1,0:T(8,128)(2,1)}, bf16[16,64,256]{2,1,0:T(8,128)(2,1)}, u32[]{:S(2)}, u32[]{:S(2)}) collective-permute-start(bf16[16,64,256]{2,1,0:T(8,128)(2,1)} %get-tuple-element.191), channel_id=1, source_target_pairs={{0,6},{1,7},{2,4},{3,5},{4,2},{5,3},{6,0},{7,1}} | collective-permute-start | bytes 1572872 | tf_op jit(solution)/shard_map/ppermute | solution.py:297
  973.2 101.6 %collective-permute-start.53 = (bf16[16,64,256]{2,1,0:T(8,128)(2,1)}, bf16[16,64,256]{2,1,0:T(8,128)(2,1)}, u32[]{:S(2)}, u32[]{:S(2)}) collective-permute-start(bf16[16,64,256]{2,1,0:T(8,128)(2,1)} %get-tuple-element.192), channel_id=1, source_target_pairs={{0,7},{1,6},{2,5},{3,4},{4,3},{5,2},{6,1},{7,0}} | collective-permute-start | bytes 1572872 | tf_op jit(solution)/shard_map/ppermute | solution.py:297
  987.3 105.7 %collective-permute-start.79 = (bf16[16,64,256]{2,1,0:T(8,128)(2,1)}, bf16[16,64,256]{2,1,0:T(8,128)(2,1)}, u32[]{:S(2)}, u32[]{:S(2)}) collective-permute-start(bf16[16,64,256]{2,1,0:T(8,128)(2,1)} %get-tuple-element.228), channel_id=1, source_target_pairs={{0,1},{1,0},{2,3},{3,2},{4,5},{5,4},{6,7},{7,6}} | collective-permute-start | bytes 1572872 | tf_op jit(solution)/shard_map/ppermute | solution.py:297
  (215 other events, 4568.0 us)
where the time goes:
time: 1130 us
  waiting for transfers between devices  467 us (41%)
  Pallas kernels  394 us (35%)
  local copies, waits for them, and re-layouts  167 us (15%)
  starting transfers between devices  80.3 us (7%)
  other arithmetic  19.9 us (2%)
    ppermute x86, waiting for transfers between devices, swap(): return lax.ppermute(x, ('lon', 'lat'), [(s, s ^ t) for s in range(nd)])  467 us
    pallas_call x30, Pallas kernels, call(): return lambda *args: fn(*args, *deps)  394 us
    unnamed x323, local copies, waits for them, and re-layouts  117 us
    ppermute x86, starting transfers between devices, swap(): return lax.ppermute(x, ('lon', 'lat'), [(s, s ^ t) for s in range(nd)])  80.3 us
    dynamic_slice x1, local copies, waits for them, and re-layouts, local_layer(): lax.dynamic_index_in_dim(w, h, axis=1, keepdims=False)  26.7 us
    squeeze x1, local copies, waits for them, and re-layouts, local_layer(): w[:, :, x * oh:(x + 1) * oh, p]  23 us
  transfers between devices with their start and end apart: 86, of which 23 were waited for; matrix products, arithmetic and copies ran while one was open for 8% of the time, Pallas kernels for 34%

commit v1 on v0

--- a/solution.py
+++ b/solution.py
@@ -17,7 +17,7 @@
 PAD = LB + 1
 MG = 64
 NV = 4
-MIX = ((1, 0), (3,), (2,))
+MIX = ((1, 0), (3, 2))
 NT = (((1,), (1,)), ((), ()))
 TN = (((0,), (0,)), ((), ()))
 
@@ -252,7 +252,7 @@
     lax.fori_loop(0, buf.shape[0], body, 0)
 
 
-def call(kernel, grid, in_specs, out_specs, out_shape, flops, nbytes, scratch=(), deps=(), alias=None, vmem=32):
+def call(kernel, grid, in_specs, out_specs, out_shape, flops, nbytes, scratch=(), deps=(), alias=None):
     fn = pl.pallas_call(
         kernel,
         grid_spec=pltpu.PrefetchScalarGridSpec(
@@ -261,7 +261,7 @@
             out_specs=out_specs, scratch_shapes=list(scratch)),
         out_shape=out_shape,
         input_output_aliases=alias or {},
-        compiler_params=pltpu.CompilerParams(dimension_semantics=("arbitrary",) * len(grid), vmem_limit_bytes=vmem * 2 ** 20),
+        compiler_params=pltpu.CompilerParams(dimension_semantics=("arbitrary",) * len(grid), vmem_limit_bytes=58 * 2 ** 20),
         cost_estimate=pl.CostEstimate(flops=int(flops), bytes_accessed=int(nbytes), transcendentals=0),
     )
     return lambda *args: fn(*args, *deps)
@@ -315,7 +315,7 @@
                 [pl.BlockSpec((1, 1, 1, cb, row_count, col_count),
                               functools.partial(lambda t, i, s: ((s[0] ^ t) // 2, half, (s[0] ^ t) % 2, base + i, 0, 0), t)) for t in range(nd)],
                 [pl.BlockSpec((cb, row_count, col_count), lambda i, s: (i, 0, 0))] * nd,
-                [piece(cc)] * nd, 1e6, nd * cc * row_count * col_count * 6, vmem=16)(scal, *([f6] * nd))
+                [piece(cc)] * nd, 1e6, nd * cc * row_count * col_count * 6)(scal, *([f6] * nd))
 
         def dft_chunk(pieces, cc, nb, deps):
             return call(
@@ -338,7 +338,7 @@
                 functools.partial(fwd_leg_kernel, len(fs)), (n_deg // MB,),
                 tri_specs + [f_spec(f.shape[1]) for f in fs],
                 spec_specs * 2, spec_shapes * 2,
-                1.3 * n_deg * n_deg * n_lat * half_c, 50e6, vmem=26)(scal, *pw, *fs)
+                1.3 * n_deg * n_deg * n_lat * half_c, 50e6)(scal, *pw, *fs)
             return res[:NV], res[NV:]
 
         def leg_inv(offs, ccs, mine, recv):
@@ -347,7 +347,7 @@
                 tri_specs + spec_specs * 2,
                 [f_spec(cc) for cc in ccs],
                 [jax.ShapeDtypeStruct((nms, cc, n_lat), BF) for cc in ccs],
-                1.3 * n_deg * n_deg * n_lat * half_c, 50e6, vmem=26)(scal, *pi, *mine, *recv)
+                1.3 * n_deg * n_deg * n_lat * half_c, 50e6)(scal, *pi, *mine, *recv)
 
         sizes = HALVES[0] + HALVES[1]
         starts = [(half, sum(part[:k])) for half, part in enumerate(HALVES) for k in range(len(part))]
@@ -396,7 +396,7 @@
             return call(
                 functools.partial(mix_kernel, vs), (2 * len(vs),), [w_spec, w_spec] + specs, outs, shapes,
                 4.0 * 4 * LB * MG * (vs[0] + 1) * channels * channels, 40e6,
-                [pltpu.VMEM((4, rows, 128), F32), pltpu.VMEM((2, rows, 128), F32)], vmem=40)(scal, *w_parts[out_half], *args)
+                [pltpu.VMEM((4, rows, 128), F32), pltpu.VMEM((2, rows, 128), F32)])(scal, *w_parts[out_half], *args)
 
         def mix_half(half):
             mine, recv = [None] * NV, [None] * NV
@@ -429,7 +429,7 @@
                 final_kernel, (nd, nb), [big] + [own(n) for n in range(nd)], big,
                 jax.ShapeDtypeStruct(f6.shape, F32), 40 * nd * cc * row_count * col_count, 10 * nd * cc * row_count * col_count,
                 [pltpu.VMEM((cb, row_count, col_count), BF)], deps,
-                {2 + nd: 0} if deps else None, 16)(scal, f6, *pieces)
+                {2 + nd: 0} if deps else None)(scal, f6, *pieces)
 
         k = 0
         out = None

time: 1130 us -> 1120 us (level)
  local copies, waits for them, and re-layouts: 167 us -> 83.2 us
  Pallas kernels: 394 us -> 446 us
  waiting for transfers between devices: 467 us -> 485 us
    unnamed x323 -> x95, local copies, waits for them, and re-layouts: 117 us -> 33.1 us
    pallas_call x30 -> x28, Pallas kernels: 394 us -> 446 us  [call(): return lambda *args: fn(*args, *deps)]
    ppermute x86, waiting for transfers between devices: 467 us -> 485 us  [swap(): return lax.ppermute(x, ('lon', 'lat'), [(s, s ^ t) for s in range(nd)])]
  transfers between devices with their start and end apart: 86 -> 86, of which waited for: 23 -> 22; matrix products, arithmetic and copies ran while one was open for 8% -> 8% of each run, Pallas kernels for 34% -> 40%
where the time goes in v1:
time: 1120 us; the launch traced here: 1110 us
  waiting for transfers between devices  485 us (43%)
  Pallas kernels  446 us (40%)
  local copies, waits for them, and re-layouts  83.2 us (7%)
  starting transfers between devices  79.2 us (7%)
  other arithmetic  20.4 us (2%)
    ppermute x86, waiting for transfers between devices, swap(): return lax.ppermute(x, ('lon', 'lat'), [(s, s ^ t) for s in range(nd)])  485 us
    pallas_call x28, Pallas kernels, call(): return lambda *args: fn(*args, *deps)  446 us
    ppermute x86, starting transfers between devices, swap(): return lax.ppermute(x, ('lon', 'lat'), [(s, s ^ t) for s in range(nd)])  79.2 us
    unnamed x95, local copies, waits for them, and re-layouts  33.1 us
    dynamic_slice x1, local copies, waits for them, and re-layouts, local_layer(): lax.dynamic_index_in_dim(w, h, axis=1, keepdims=False)  26.7 us
    squeeze x1, local copies, waits for them, and re-layouts, local_layer(): w[:, :, x * oh:(x + 1) * oh, p]  23.4 us
  transfers between devices with their start and end apart: 86, of which 22 were waited for; matrix products, arithmetic and copies ran while one was open for 8% of the time, Pallas kernels for 40%

profile of v1, /device:TPU:0, one launch (start us, length us, event | category | flops | bytes accessed | tf_op | source)
XLA Modules:
  0.0 1114.2 jit_solution(913089876015360518)
XLA Ops:
  36.4 21.1 %collective-permute-done.4.refs_5_ = bf16[16,64,256]{2,1,0:T(8,128)(2,1)} collective-permute-done((bf16[16,64,256]{2,1,0:T(8,128)(2,1)}, bf16[16,64,256]{2,1,0:T(8,128)(2,1)}, u32[]{:S(2)}, u32[]{:S(2)}) %collective-permute-start.4) | collective-permute-done | bytes 524320 | tf_op jit(solution)/shard_map/ppermute | solution.py:297
  115.4 26.7 %constant_dynamic-slice_fusion = bf16[8,1,16,256,256,2]{4,5,3,2,1,0:T(2,128)(2,1)} fusion(bf16[8,2,16,256,256,2]{4,5,3,2,1,0:T(2,128)(2,1)} %bitcast.5, s32[]{:T(128)S(6)} %select_n.133), kind=kLoop, calls=%fused_computation.68 | loop fusion | bytes 67108864 | tf_op jit(solution)/shard_map/jit(dynamic_index_in_dim)/dynamic_slice | solution.py:361
  142.1 22.7 %copy.17 = bf16[8,1,16,256,256,2]{4,3,2,0,5,1:T(8,128)(2,1)} copy(bf16[8,1,16,256,256,2]{4,5,3,2,1,0:T(2,128)(2,1)} %constant_dynamic-slice_fusion) | data formatting | bytes 67108864
  164.8 18.3 %collective-permute-done.29.refs_2_ = bf16[16,64,256]{2,1,0:T(8,128)(2,1)} collective-permute-done((bf16[16,64,256]{2,1,0:T(8,128)(2,1)}, bf16[16,64,256]{2,1,0:T(8,128)(2,1)}, u32[]{:S(2)}, u32[]{:S(2)}) %collective-permute-start.29) | collective-permute-done | bytes 524320 | tf_op jit(solution)/shard_map/ppermute | solution.py:297
  187.8 23.4 %slice_bitcast_fusion = (bf16[128,256,128]{2,1,0:T(8,128)(2,1)}, bf16[128,256,128]{2,1,0:T(8,128)(2,1)}, bf16[128,256,128]{2,1,0:T(8,128)(2,1)}, bf16[128,256,128]{2,1,0:T(8,128)(2,1)}) fusion(bf16[128,256,256,2]{2,1,0,3:T(8,128)(2,1)} %bitcast.64), kind=kLoop, calls=%fused_computation | loop fusion | bytes 67108864 | tf_op jit(solution)/shard_map/squeeze | solution.py:363
  222.5 65.1 %collective-permute-done.10.refs_4_ = bf16[48,64,256]{2,1,0:T(8,128)(2,1)} collective-permute-done((bf16[48,64,256]{2,1,0:T(8,128)(2,1)}, bf16[48,64,256]{2,1,0:T(8,128)(2,1)}, u32[]{:S(2)}, u32[]{:S(2)}) %collective-permute-start.10) | collective-permute-done | bytes 1572896 | tf_op jit(solution)/shard_map/ppermute | solution.py:297
  290.2 31.4 %collective-permute-done.11.refs_5_ = bf16[48,64,256]{2,1,0:T(8,128)(2,1)} collective-permute-done((bf16[48,64,256]{2,1,0:T(8,128)(2,1)}, bf16[48,64,256]{2,1,0:T(8,128)(2,1)}, u32[]{:S(2)}, u32[]{:S(2)}) %collective-permute-start.11) | collective-permute-done | bytes 1572896 | tf_op jit(solution)/shard_map/ppermute | solution.py:297
  325.2 19.6 %shard_map.121.refs_5_.refs_8_ = bf16[512,48,256]{2,1,0:T(8,128)(2,1)} custom-call(s32[4]{0:T(128)} %pad_add_fusion.s_ref, bf16[2,512,512]{2,1,0:T(8,128)(2,1)} %constant.166.clone.tab_ref, bf16[48,64,256]{2,1,0:T(8,128)(2,1)} %get-tuple-element.128.refs_0_, bf16[48,64,256]{2,1,0:T(8,128)(2,1)} %copy-done.11, bf16[48,64,256]{2,1,0:T(8,128)(2,1)} %copy-done.12, ...), custom_call_target="tpu_custom_call" | custom-call | flops 12884901888 | bytes 37748736 | tf_op jit(solution)/shard_map/pallas_call | solution.py:267
  344.8 21.3 %shard_map.122 = (bf16[2,64,16,128]{3,2,1,0:T(8,128)(2,1)}, bf16[2,128,16,128]{3,2,1,0:T(8,128)(2,1)}, bf16[2,192,16,128]{3,2,1,0:T(8,128)(2,1)}, bf16[2,256,16,...) custom-call(s32[4]{0:T(128)} %pad_add_fusion.s_ref, ...), custom_call_target="tpu_custom_call" | custom-call | flops 2791728640 | bytes 50000000 | tf_op jit(solution)/shard_map/pallas_call | solution.py:267
  368.2 21.2 %collective-permute-done.17.refs_4_ = bf16[32,64,256]{2,1,0:T(8,128)(2,1)} collective-permute-done((bf16[32,64,256]{2,1,0:T(8,128)(2,1)S(1)}, bf16[32,64,256]{2,1,0:T(8,128)(2,1)}, u32[]{:S(2)}, u32[]{:S(2)}) %collective-permute-start.17) | collective-permute-done | bytes 1048608 | tf_op jit(solution)/shard_map/ppermute | solution.py:297
  391.3 20.2 %collective-permute-done.18.refs_5_ = bf16[32,64,256]{2,1,0:T(8,128)(2,1)} collective-permute-done((bf16[32,64,256]{2,1,0:T(8,128)(2,1)S(1)}, bf16[32,64,256]{2,1,0:T(8,128)(2,1)}, u32[]{:S(2)}, u32[]{:S(2)}) %collective-permute-start.18) | collective-permute-done | bytes 1048608 | tf_op jit(solution)/shard_map/ppermute | solution.py:297
  415.1 15.0 %shard_map.124.refs_8_.refs_4_ = bf16[512,32,256]{2,1,0:T(8,128)(2,1)} custom-call(s32[4]{0:T(128)} %pad_add_fusion.s_ref, bf16[2,512,512]{2,1,0:T(8,128)(2,1)} %constant.166.clone.tab_ref, bf16[32,64,256]{2,1,0:T(8,128)(2,1)} %get-tuple-element.137.refs_0_, bf16[32,64,256]{2,1,0:T(8,128)(2,1)} %collective-permute-done.14.refs_1_, ...), custom_call_target="tpu_custom_call" | custom-call | flops 8589934592 | bytes 25165824 | tf_op jit(solution)/shard_map/pallas_call | solution.py:267
  466.3 21.1 %shard_map.129 = (bf16[2,64,16,128]{3,2,1,0:T(8,128)(2,1)}, bf16[2,128,16,128]{3,2,1,0:T(8,128)(2,1)}, bf16[2,192,16,128]{3,2,1,0:T(8,128)(2,1)}, bf16[2,256,16,...) custom-call(s32[4]{0:T(128)} %pad_add_fusion.s_ref, ...), custom_call_target="tpu_custom_call" | custom-call | flops 2791728640 | bytes 50000000 | tf_op jit(solution)/shard_map/pallas_call | solution.py:267
  496.5 24.1 %shard_map.131 = (bf16[2,256,16,128]{3,2,1,0:T(8,128)(2,1)}, bf16[2,256,16,128]{3,2,1,0:T(8,128)(2,1)}, bf16[2,192,16,128]{3,2,1,0:T(8,128)(2,1)}, bf16[2,192,16,128]{3,2,1,0:T(8,128)(2,1)}) custom-call(s32[4]{0:T(128)} %pad_add_fusion.s_ref, bf16[128,256,128]{2,1,0:T(8,128)(2,1)} %get-tuple-element.238.refs_11_.wre, ...), custom_call_target="tpu_custom_call" | custom-call | flops 4294967296 | bytes 40000000 | tf_op jit(solution)/shard_map/pallas_call | solution.py:267
  520.8 15.5 %shard_map.130 = (bf16[2,128,16,128]{3,2,1,0:T(8,128)(2,1)}, bf16[2,128,16,128]{3,2,1,0:T(8,128)(2,1)}, bf16[2,64,16,128]{3,2,1,0:T(8,128)(2,1)}, bf16[2,64,16,128]{3,2,1,0:T(8,128)(2,1)}) custom-call(s32[4]{0:T(128)} %pad_add_fusion.s_ref, bf16[128,256,128]{2,1,0:T(8,128)(2,1)} %get-tuple-element.238.refs_11_.wre, ...), custom_call_target="tpu_custom_call" | custom-call | flops 2147483648 | bytes 40000000 | tf_op jit(solution)/shard_map/pallas_call | solution.py:267
  537.3 24.3 %shard_map.136 = (bf16[2,256,16,128]{3,2,1,0:T(8,128)(2,1)}, bf16[2,256,16,128]{3,2,1,0:T(8,128)(2,1)}, bf16[2,192,16,128]{3,2,1,0:T(8,128)(2,1)}, bf16[2,192,16,128]{3,2,1,0:T(8,128)(2,1)}) custom-call(s32[4]{0:T(128)} %pad_add_fusion.s_ref, bf16[128,256,128]{2,1,0:T(8,128)(2,1)} %get-tuple-element.236.refs_9_.wre, ...), custom_call_target="tpu_custom_call" | custom-call | flops 4294967296 | bytes 40000000 | tf_op jit(solution)/shard_map/pallas_call | solution.py:267
  562.2 15.4 %shard_map.135 = (bf16[2,128,16,128]{3,2,1,0:T(8,128)(2,1)}, bf16[2,128,16,128]{3,2,1,0:T(8,128)(2,1)}, bf16[2,64,16,128]{3,2,1,0:T(8,128)(2,1)}, bf16[2,64,16,128]{3,2,1,0:T(8,128)(2,1)}) custom-call(s32[4]{0:T(128)} %pad_add_fusion.s_ref, bf16[128,256,128]{2,1,0:T(8,128)(2,1)} %get-tuple-element.236.refs_9_.wre, ...), custom_call_target="tpu_custom_call" | custom-call | flops 2147483648 | bytes 40000000 | tf_op jit(solution)/shard_map/pallas_call | solution.py:267
  579.1 20.8 %shard_map.132 = (bf16[512,32,256]{2,1,0:T(8,128)(2,1)}, bf16[512,16,256]{2,1,0:T(8,128)(2,1)}, bf16[512,16,256]{2,1,0:T(8,128)(2,1)}) custom-call(s32[4]{0:T(128)} %pad_add_fusion.s_ref, bf16[64,2,32,256]{3,2,1,0:T(8,128)(2,1)} %constant.162.clone.refs_0_, bf16[128,2,32,256]{3,2,1,0:T(8,128)(2,1)} %constant.163.clone.refs_1_, ...), custom_call_target="tpu_custom_call" | custom-call | flops 2791728640 | bytes 50000000 | tf_op jit(solution)/shard_map/pallas_call | solution.py:267
  613.3 17.8 %shard_map.139.g_ref = bf16[512,16,256]{2,1,0:T(8,128)(2,1)} custom-call(s32[4]{0:T(128)} %pad_add_fusion.s_ref, bf16[64,2,32,256]{3,2,1,0:T(8,128)(2,1)} %constant.162.clone.refs_0_, bf16[128,2,32,256]{3,2,1,0:T(8,128)(2,1)} %constant.163.clone.refs_1_, bf16[192,2,32,256]{3,2,1,0:T(8,128)(2,1)} %constant.164.clone.refs_2_, ...), custom_call_target="tpu_custom_call" | custom-call | flops 2791728640 | bytes 50000000 | tf_op jit(solution)/shard_map/pallas_call | solution.py:267
  660.3 19.8 %shard_map.137.g_ref = bf16[512,48,256]{2,1,0:T(8,128)(2,1)} custom-call(s32[4]{0:T(128)} %pad_add_fusion.s_ref, bf16[64,2,32,256]{3,2,1,0:T(8,128)(2,1)} %constant.162.clone.refs_0_, bf16[128,2,32,256]{3,2,1,0:T(8,128)(2,1)} %constant.163.clone.refs_1_, bf16[192,2,32,256]{3,2,1,0:T(8,128)(2,1)} %constant.164.clone.refs_2_, ...), custom_call_target="tpu_custom_call" | custom-call | flops 2791728640 | bytes 50000000 | tf_op jit(solution)/shard_map/pallas_call | solution.py:267
  685.5 19.5 %shard_map.138 = (bf16[48,64,256]{2,1,0:T(8,128)(2,1)}, bf16[48,64,256]{2,1,0:T(8,128)(2,1)}, bf16[48,64,256]{2,1,0:T(8,128)(2,1)}, bf16[48,64,256]{2,1,0:T(8,12...) custom-call(s32[4]{0:T(128)} %pad_add_fusion.s_ref, ...), custom_call_target="tpu_custom_call" | custom-call | flops 12884901888 | bytes 37748736 | tf_op jit(solution)/shard_map/pallas_call | solution.py:267
  705.0 35.7 %collective-permute-done.78.refs_7_ = bf16[16,64,256]{2,1,0:T(8,128)(2,1)S(1)} collective-permute-done((bf16[16,64,256]{2,1,0:T(8,128)(2,1)S(1)}, bf16[16,64,256]{2,1,0:T(8,128)(2,1)S(1)}, u32[]{:S(2)}, u32[]{:S(2)}) %collective-permute-start.78) | collective-permute-done | bytes 524320 | tf_op jit(solution)/shard_map/ppermute | solution.py:297
  746.5 21.7 %collective-permute-done.58.refs_5_ = bf16[32,64,256]{2,1,0:T(8,128)(2,1)S(1)} collective-permute-done((bf16[32,64,256]{2,1,0:T(8,128)(2,1)}, bf16[32,64,256]{2,1,0:T(8,128)(2,1)S(1)}, u32[]{:S(2)}, u32[]{:S(2)}) %collective-permute-start.58) | collective-permute-done | bytes 1048608 | tf_op jit(solution)/shard_map/ppermute | solution.py:297
  769.3 33.4 %collective-permute-done.59.refs_6_ = bf16[32,64,256]{2,1,0:T(8,128)(2,1)S(1)} collective-permute-done((bf16[32,64,256]{2,1,0:T(8,128)(2,1)}, bf16[32,64,256]{2,1,0:T(8,128)(2,1)S(1)}, u32[]{:S(2)}, u32[]{:S(2)}) %collective-permute-start.59) | collective-permute-done | bytes 1048608 | tf_op jit(solution)/shard_map/ppermute | solution.py:297
  803.3 20.5 %collective-permute-done.60.refs_7_ = bf16[32,64,256]{2,1,0:T(8,128)(2,1)S(1)} collective-permute-done((bf16[32,64,256]{2,1,0:T(8,128)(2,1)}, bf16[32,64,256]{2,1,0:T(8,128)(2,1)S(1)}, u32[]{:S(2)}, u32[]{:S(2)}) %collective-permute-start.60) | collective-permute-done | bytes 1048608 | tf_op jit(solution)/shard_map/ppermute | solution.py:297
  827.4 29.3 %collective-permute-done.67.refs_3_ = bf16[48,64,256]{2,1,0:T(8,128)(2,1)} collective-permute-done((bf16[48,64,256]{2,1,0:T(8,128)(2,1)}, bf16[48,64,256]{2,1,0:T(8,128)(2,1)}, u32[]{:S(2)}, u32[]{:S(2)}) %collective-permute-start.67) | collective-permute-done | bytes 1572896 | tf_op jit(solution)/shard_map/ppermute | solution.py:297
  859.6 99.6 %collective-permute-done.69.refs_5_ = bf16[48,64,256]{2,1,0:T(8,128)(2,1)} collective-permute-done((bf16[48,64,256]{2,1,0:T(8,128)(2,1)}, bf16[48,64,256]{2,1,0:T(8,128)(2,1)}, u32[]{:S(2)}, u32[]{:S(2)}) %collective-permute-start.69) | collective-permute-done | bytes 1572896 | tf_op jit(solution)/shard_map/ppermute | solution.py:297
  973.2 15.1 %shard_map.141.refs_8_ = f32[4,2,2,64,64,256]{5,4,3,2,1,0:T(8,128)} custom-call(s32[4]{0:T(128)} %pad_add_fusion.s_ref, f32[4,2,2,64,64,256]{5,4,3,2,1,0:T(8,128)} %bitcast.4.refs_0_.refs_1_.refs_2_.refs_3_.refs_4_.refs_5_.refs_6_.refs_7_.f_ref, bf16[16,64,256]{2,1,0:T(8,128)(2,1)} %get-tuple-element.218.refs_0_, ...), custom_call_target="tpu_custom_call" | custom-call | flops 83886080 | bytes 20971520 | tf_op jit(solution)/shard_map/pallas_call | solution.py:267
  988.3 40.8 %shard_map.142.refs_8_ = f32[4,2,2,64,64,256]{5,4,3,2,1,0:T(8,128)} custom-call(s32[4]{0:T(128)} %pad_add_fusion.s_ref, f32[4,2,2,64,64,256]{5,4,3,2,1,0:T(8,128)} %bitcast.4.refs_0_.refs_1_.refs_2_.refs_3_.refs_4_.refs_5_.refs_6_.refs_7_.f_ref, bf16[48,64,256]{2,1,0:T(8,128)(2,1)} %get-tuple-element.210.refs_0_, ...), custom_call_target="tpu_custom_call", output_to_operand_aliasing={{}: (10, {})} | custom-call | flops 251658240 | bytes 62914560 | tf_op jit(solution)/shard_map/pallas_call | solution.py:267
  1029.2 28.1 %shard_map.143.refs_8_ = f32[4,2,2,64,64,256]{5,4,3,2,1,0:T(8,128)} custom-call(s32[4]{0:T(128)} %pad_add_fusion.s_ref, f32[4,2,2,64,64,256]{5,4,3,2,1,0:T(8,128)} %bitcast.4.refs_0_.refs_1_.refs_2_.refs_3_.refs_4_.refs_5_.refs_6_.refs_7_.f_ref, bf16[32,64,256]{2,1,0:T(8,128)(2,1)} %get-tuple-element.194.refs_0_, ...), custom_call_target="tpu_custom_call", output_to_operand_aliasing={{}: (10, {})} | custom-call | flops 167772160 | bytes 41943040 | tf_op jit(solution)/shard_map/pallas_call | solution.py:267
  1060.8 15.2 %shard_map.144 = f32[4,2,2,64,64,256]{5,4,3,2,1,0:T(8,128)} custom-call(s32[4]{0:T(128)} %pad_add_fusion.s_ref, f32[4,2,2,64,64,256]{5,4,3,2,1,0:T(8,128)} %bitcast.4.refs_0_.refs_1_.refs_2_.refs_3_.refs_4_.refs_5_.refs_6_.refs_7_.f_ref, bf16[16,64,256]{2,1,0:T(8,128)(2,1)} %get-tuple-element.185.refs_0_, ...), custom_call_target="tpu_custom_call", output_to_operand_aliasing={{}: (10, {})} | custom-call | flops 83886080 | bytes 20971520 | tf_op jit(solution)/shard_map/pallas_call | solution.py:267
  1090.8 16.0 %collective-permute-done.83 = bf16[16,64,256]{2,1,0:T(8,128)(2,1)S(1)} collective-permute-done((bf16[16,64,256]{2,1,0:T(8,128)(2,1)S(1)}, bf16[16,64,256]{2,1,0:T(8,128)(2,1)S(1)}, u32[]{:S(2)}, u32[]{:S(2)}) %collective-permute-start.83) | collective-permute-done | bytes 524320 | tf_op jit(solution)/shard_map/ppermute | solution.py:297
  (274 shorter events, 273.8 us)
Async XLA Ops:
  103.2 82.3 %collective-permute-start.7 = (bf16[48,64,256]{2,1,0:T(8,128)(2,1)}, bf16[48,64,256]{2,1,0:T(8,128)(2,1)S(1)}, u32[]{:S(2)}, u32[]{:S(2)}) collective-permute-start(bf16[48,64,256]{2,1,0:T(8,128)(2,1)} %get-tuple-element.129), channel_id=1, source_target_pairs={{0,1},{1,0},{2,3},{3,2},{4,5},{5,4},{6,7},{7,6}} | collective-permute-start | bytes 4718600 | tf_op jit(solution)/shard_map/ppermute | solution.py:297
  112.2 75.4 %collective-permute-start.8 = (bf16[48,64,256]{2,1,0:T(8,128)(2,1)}, bf16[48,64,256]{2,1,0:T(8,128)(2,1)S(1)}, u32[]{:S(2)}, u32[]{:S(2)}) collective-permute-start(bf16[48,64,256]{2,1,0:T(8,128)(2,1)} %get-tuple-element.130), channel_id=1, source_target_pairs={{0,2},{1,3},{2,0},{3,1},{4,6},{5,7},{6,4},{7,5}} | collective-permute-start | bytes 4718600 | tf_op jit(solution)/shard_map/ppermute | solution.py:297
  113.0 70.4 %collective-permute-start.14 = (bf16[32,64,256]{2,1,0:T(8,128)(2,1)}, bf16[32,64,256]{2,1,0:T(8,128)(2,1)}, u32[]{:S(2)}, u32[]{:S(2)}) collective-permute-start(bf16[32,64,256]{2,1,0:T(8,128)(2,1)} %get-tuple-element.138), channel_id=1, source_target_pairs={{0,1},{1,0},{2,3},{3,2},{4,5},{5,4},{6,7},{7,6}} | collective-permute-start | bytes 3145736 | tf_op jit(solution)/shard_map/ppermute | solution.py:297
  113.4 71.8 %collective-permute-start.15 = (bf16[32,64,256]{2,1,0:T(8,128)(2,1)}, bf16[32,64,256]{2,1,0:T(8,128)(2,1)}, u32[]{:S(2)}, u32[]{:S(2)}) collective-permute-start(bf16[32,64,256]{2,1,0:T(8,128)(2,1)} %get-tuple-element.139), channel_id=1, source_target_pairs={{0,2},{1,3},{2,0},{3,1},{4,6},{5,7},{6,4},{7,5}} | collective-permute-start | bytes 3145736 | tf_op jit(solution)/shard_map/ppermute | solution.py:297
  114.5 68.6 %collective-permute-start.29 = (bf16[16,64,256]{2,1,0:T(8,128)(2,1)}, bf16[16,64,256]{2,1,0:T(8,128)(2,1)}, u32[]{:S(2)}, u32[]{:S(2)}) collective-permute-start(bf16[16,64,256]{2,1,0:T(8,128)(2,1)} %get-tuple-element.156), channel_id=1, source_target_pairs={{0,2},{1,3},{2,0},{3,1},{4,6},{5,7},{6,4},{7,5}} | collective-permute-start | bytes 1572872 | tf_op jit(solution)/shard_map/ppermute | solution.py:297
  183.4 104.3 %collective-permute-start.10 = (bf16[48,64,256]{2,1,0:T(8,128)(2,1)}, bf16[48,64,256]{2,1,0:T(8,128)(2,1)}, u32[]{:S(2)}, u32[]{:S(2)}) collective-permute-start(bf16[48,64,256]{2,1,0:T(8,128)(2,1)} %get-tuple-element.132), channel_id=1, source_target_pairs={{0,4},{1,5},{2,6},{3,7},{4,0},{5,1},{6,2},{7,3}} | collective-permute-start | bytes 4718600 | tf_op jit(solution)/shard_map/ppermute | solution.py:297
  185.2 136.4 %collective-permute-start.11 = (bf16[48,64,256]{2,1,0:T(8,128)(2,1)}, bf16[48,64,256]{2,1,0:T(8,128)(2,1)}, u32[]{:S(2)}, u32[]{:S(2)}) collective-permute-start(bf16[48,64,256]{2,1,0:T(8,128)(2,1)} %get-tuple-element.133), channel_id=1, source_target_pairs={{0,5},{1,4},{2,7},{3,6},{4,1},{5,0},{6,3},{7,2}} | collective-permute-start | bytes 4718600 | tf_op jit(solution)/shard_map/ppermute | solution.py:297
  185.4 137.9 %collective-permute-start.12 = (bf16[48,64,256]{2,1,0:T(8,128)(2,1)}, bf16[48,64,256]{2,1,0:T(8,128)(2,1)}, u32[]{:S(2)}, u32[]{:S(2)}) collective-permute-start(bf16[48,64,256]{2,1,0:T(8,128)(2,1)} %get-tuple-element.134), channel_id=1, source_target_pairs={{0,6},{1,7},{2,4},{3,5},{4,2},{5,3},{6,0},{7,1}} | collective-permute-start | bytes 4718600 | tf_op jit(solution)/shard_map/ppermute | solution.py:297
  187.6 136.4 %collective-permute-start.13 = (bf16[48,64,256]{2,1,0:T(8,128)(2,1)}, bf16[48,64,256]{2,1,0:T(8,128)(2,1)}, u32[]{:S(2)}, u32[]{:S(2)}) collective-permute-start(bf16[48,64,256]{2,1,0:T(8,128)(2,1)} %get-tuple-element.135), channel_id=1, source_target_pairs={{0,7},{1,6},{2,5},{3,4},{4,3},{5,2},{6,1},{7,0}} | collective-permute-start | bytes 4718600 | tf_op jit(solution)/shard_map/ppermute | solution.py:297
  221.5 144.7 %collective-permute-start.16 = (bf16[32,64,256]{2,1,0:T(8,128)(2,1)}, bf16[32,64,256]{2,1,0:T(8,128)(2,1)}, u32[]{:S(2)}, u32[]{:S(2)}) collective-permute-start(bf16[32,64,256]{2,1,0:T(8,128)(2,1)} %get-tuple-element.140), channel_id=1, source_target_pairs={{0,3},{1,2},{2,1},{3,0},{4,7},{5,6},{6,5},{7,4}} | collective-permute-start | bytes 3145736 | tf_op jit(solution)/shard_map/ppermute | solution.py:297
  287.7 101.8 %collective-permute-start.17 = (bf16[32,64,256]{2,1,0:T(8,128)(2,1)S(1)}, bf16[32,64,256]{2,1,0:T(8,128)(2,1)}, u32[]{:S(2)}, u32[]{:S(2)}) collective-permute-start(bf16[32,64,256]{2,1,0:T(8,128)(2,1)S(1)} %copy-done.32), channel_id=1, source_target_pairs={{0,4},{1,5},{2,6},{3,7},{4,0},{5,1},{6,2},{7,3}} | collective-permute-start | bytes 3145736 | tf_op jit(solution)/shard_map/ppermute | solution.py:297
  321.6 89.9 %collective-permute-start.18 = (bf16[32,64,256]{2,1,0:T(8,128)(2,1)S(1)}, bf16[32,64,256]{2,1,0:T(8,128)(2,1)}, u32[]{:S(2)}, u32[]{:S(2)}) collective-permute-start(bf16[32,64,256]{2,1,0:T(8,128)(2,1)S(1)} %copy-done.31), channel_id=1, source_target_pairs={{0,5},{1,4},{2,7},{3,6},{4,1},{5,0},{6,3},{7,2}} | collective-permute-start | bytes 3145736 | tf_op jit(solution)/shard_map/ppermute | solution.py:297
  323.3 89.9 %collective-permute-start.19 = (bf16[32,64,256]{2,1,0:T(8,128)(2,1)S(1)}, bf16[32,64,256]{2,1,0:T(8,128)(2,1)}, u32[]{:S(2)}, u32[]{:S(2)}) collective-permute-start(bf16[32,64,256]{2,1,0:T(8,128)(2,1)S(1)} %copy-done.30), channel_id=1, source_target_pairs={{0,6},{1,7},{2,4},{3,5},{4,2},{5,3},{6,0},{7,1}} | collective-permute-start | bytes 3145736 | tf_op jit(solution)/shard_map/ppermute | solution.py:297
  324.0 89.9 %collective-permute-start.20 = (bf16[32,64,256]{2,1,0:T(8,128)(2,1)S(1)}, bf16[32,64,256]{2,1,0:T(8,128)(2,1)}, u32[]{:S(2)}, u32[]{:S(2)}) collective-permute-start(bf16[32,64,256]{2,1,0:T(8,128)(2,1)S(1)} %copy-done.29), channel_id=1, source_target_pairs={{0,7},{1,6},{2,5},{3,4},{4,3},{5,2},{6,1},{7,0}} | collective-permute-start | bytes 3145736 | tf_op jit(solution)/shard_map/ppermute | solution.py:297
  366.1 73.6 %collective-permute-start.30 = (bf16[16,64,256]{2,1,0:T(8,128)(2,1)S(1)}, bf16[16,64,256]{2,1,0:T(8,128)(2,1)S(1)}, u32[]{:S(2)}, u32[]{:S(2)}) collective-permute-start(bf16[16,64,256]{2,1,0:T(8,128)(2,1)S(1)} %copy-done.40), channel_id=1, source_target_pairs={{0,3},{1,2},{2,1},{3,0},{4,7},{5,6},{6,5},{7,4}} | collective-permute-start | bytes 1572872 | tf_op jit(solution)/shard_map/ppermute | solution.py:297
  680.9 61.0 %collective-permute-start.54 = (bf16[32,64,256]{2,1,0:T(8,128)(2,1)S(1)}, bf16[32,64,256]{2,1,0:T(8,128)(2,1)S(1)}, u32[]{:S(2)}, u32[]{:S(2)}) collective-permute-start(bf16[32,64,256]{2,1,0:T(8,128)(2,1)S(1)} %copy-done.33), channel_id=1, source_target_pairs={{0,1},{1,0},{2,3},{3,2},{4,5},{5,4},{6,7},{7,6}} | collective-permute-start | bytes 3145736 | tf_op jit(solution)/shard_map/ppermute | solution.py:297
  681.7 60.9 %collective-permute-start.55 = (bf16[32,64,256]{2,1,0:T(8,128)(2,1)}, bf16[32,64,256]{2,1,0:T(8,128)(2,1)S(1)}, u32[]{:S(2)}, u32[]{:S(2)}) collective-permute-start(bf16[32,64,256]{2,1,0:T(8,128)(2,1)} %get-tuple-element.196), channel_id=1, source_target_pairs={{0,2},{1,3},{2,0},{3,1},{4,6},{5,7},{6,4},{7,5}} | collective-permute-start | bytes 3145736 | tf_op jit(solution)/shard_map/ppermute | solution.py:297
  682.5 61.2 %collective-permute-start.56 = (bf16[32,64,256]{2,1,0:T(8,128)(2,1)}, bf16[32,64,256]{2,1,0:T(8,128)(2,1)}, u32[]{:S(2)}, u32[]{:S(2)}) collective-permute-start(bf16[32,64,256]{2,1,0:T(8,128)(2,1)} %get-tuple-element.197), channel_id=1, source_target_pairs={{0,3},{1,2},{2,1},{3,0},{4,7},{5,6},{6,5},{7,4}} | collective-permute-start | bytes 3145736 | tf_op jit(solution)/shard_map/ppermute | solution.py:297
  683.6 61.3 %collective-permute-start.57 = (bf16[32,64,256]{2,1,0:T(8,128)(2,1)}, bf16[32,64,256]{2,1,0:T(8,128)(2,1)}, u32[]{:S(2)}, u32[]{:S(2)}) collective-permute-start(bf16[32,64,256]{2,1,0:T(8,128)(2,1)} %get-tuple-element.198), channel_id=1, source_target_pairs={{0,4},{1,5},{2,6},{3,7},{4,0},{5,1},{6,2},{7,3}} | collective-permute-start | bytes 3145736 | tf_op jit(solution)/shard_map/ppermute | solution.py:297
  741.6 83.7 %collective-permute-start.65 = (bf16[48,64,256]{2,1,0:T(8,128)(2,1)}, bf16[48,64,256]{2,1,0:T(8,128)(2,1)S(1)}, u32[]{:S(2)}, u32[]{:S(2)}) collective-permute-start(bf16[48,64,256]{2,1,0:T(8,128)(2,1)} %get-tuple-element.211), channel_id=1, source_target_pairs={{0,1},{1,0},{2,3},{3,2},{4,5},{5,4},{6,7},{7,6}} | collective-permute-start | bytes 4718600 | tf_op jit(solution)/shard_map/ppermute | solution.py:297
  741.9 85.1 %collective-permute-start.66 = (bf16[48,64,256]{2,1,0:T(8,128)(2,1)}, bf16[48,64,256]{2,1,0:T(8,128)(2,1)S(1)}, u32[]{:S(2)}, u32[]{:S(2)}) collective-permute-start(bf16[48,64,256]{2,1,0:T(8,128)(2,1)} %get-tuple-element.212), channel_id=1, source_target_pairs={{0,2},{1,3},{2,0},{3,1},{4,6},{5,7},{6,4},{7,5}} | collective-permute-start | bytes 4718600 | tf_op jit(solution)/shard_map/ppermute | solution.py:297
  743.7 59.0 %collective-permute-start.59 = (bf16[32,64,256]{2,1,0:T(8,128)(2,1)}, bf16[32,64,256]{2,1,0:T(8,128)(2,1)S(1)}, u32[]{:S(2)}, u32[]{:S(2)}) collective-permute-start(bf16[32,64,256]{2,1,0:T(8,128)(2,1)} %get-tuple-element.200), channel_id=1, source_target_pairs={{0,6},{1,7},{2,4},{3,5},{4,2},{5,3},{6,0},{7,1}} | collective-permute-start | bytes 3145736 | tf_op jit(solution)/shard_map/ppermute | solution.py:297
  744.9 78.9 %collective-permute-start.60 = (bf16[32,64,256]{2,1,0:T(8,128)(2,1)}, bf16[32,64,256]{2,1,0:T(8,128)(2,1)S(1)}, u32[]{:S(2)}, u32[]{:S(2)}) collective-permute-start(bf16[32,64,256]{2,1,0:T(8,128)(2,1)} %get-tuple-element.201), channel_id=1, source_target_pairs={{0,7},{1,6},{2,5},{3,4},{4,3},{5,2},{6,1},{7,0}} | collective-permute-start | bytes 3145736 | tf_op jit(solution)/shard_map/ppermute | solution.py:297
  768.2 88.5 %collective-permute-start.67 = (bf16[48,64,256]{2,1,0:T(8,128)(2,1)}, bf16[48,64,256]{2,1,0:T(8,128)(2,1)}, u32[]{:S(2)}, u32[]{:S(2)}) collective-permute-start(bf16[48,64,256]{2,1,0:T(8,128)(2,1)} %get-tuple-element.213), channel_id=1, source_target_pairs={{0,3},{1,2},{2,1},{3,0},{4,7},{5,6},{6,5},{7,4}} | collective-permute-start | bytes 4718600 | tf_op jit(solution)/shard_map/ppermute | solution.py:297
  823.8 135.5 %collective-permute-start.69 = (bf16[48,64,256]{2,1,0:T(8,128)(2,1)}, bf16[48,64,256]{2,1,0:T(8,128)(2,1)}, u32[]{:S(2)}, u32[]{:S(2)}) collective-permute-start(bf16[48,64,256]{2,1,0:T(8,128)(2,1)} %get-tuple-element.215), channel_id=1, source_target_pairs={{0,5},{1,4},{2,7},{3,6},{4,1},{5,0},{6,3},{7,2}} | collective-permute-start | bytes 4718600 | tf_op jit(solution)/shard_map/ppermute | solution.py:297
  825.2 134.8 %collective-permute-start.70 = (bf16[48,64,256]{2,1,0:T(8,128)(2,1)}, bf16[48,64,256]{2,1,0:T(8,128)(2,1)}, u32[]{:S(2)}, u32[]{:S(2)}) collective-permute-start(bf16[48,64,256]{2,1,0:T(8,128)(2,1)} %get-tuple-element.216), channel_id=1, source_target_pairs={{0,6},{1,7},{2,4},{3,5},{4,2},{5,3},{6,0},{7,1}} | collective-permute-start | bytes 4718600 | tf_op jit(solution)/shard_map/ppermute | solution.py:297
  826.9 144.5 %collective-permute-start.71 = (bf16[48,64,256]{2,1,0:T(8,128)(2,1)}, bf16[48,64,256]{2,1,0:T(8,128)(2,1)S(1)}, u32[]{:S(2)}, u32[]{:S(2)}) collective-permute-start(bf16[48,64,256]{2,1,0:T(8,128)(2,1)} %get-tuple-element.217), channel_id=1, source_target_pairs={{0,7},{1,6},{2,5},{3,4},{4,3},{5,2},{6,1},{7,0}} | collective-permute-start | bytes 4718600 | tf_op jit(solution)/shard_map/ppermute | solution.py:297
  856.6 200.7 %collective-permute-start.50 = (bf16[16,64,256]{2,1,0:T(8,128)(2,1)}, bf16[16,64,256]{2,1,0:T(8,128)(2,1)}, u32[]{:S(2)}, u32[]{:S(2)}) collective-permute-start(bf16[16,64,256]{2,1,0:T(8,128)(2,1)} %get-tuple-element.189), channel_id=1, source_target_pairs={{0,4},{1,5},{2,6},{3,7},{4,0},{5,1},{6,2},{7,3}} | collective-permute-start | bytes 1572872 | tf_op jit(solution)/shard_map/ppermute | solution.py:297
  859.1 199.1 %collective-permute-start.51 = (bf16[16,64,256]{2,1,0:T(8,128)(2,1)}, bf16[16,64,256]{2,1,0:T(8,128)(2,1)}, u32[]{:S(2)}, u32[]{:S(2)}) collective-permute-start(bf16[16,64,256]{2,1,0:T(8,128)(2,1)} %get-tuple-element.190), channel_id=1, source_target_pairs={{0,5},{1,4},{2,7},{3,6},{4,1},{5,0},{6,3},{7,2}} | collective-permute-start | bytes 1572872 | tf_op jit(solution)/shard_map/ppermute | solution.py:297
  959.2 99.4 %collective-permute-start.52 = (bf16[16,64,256]{2,1,0:T(8,128)(2,1)}, bf16[16,64,256]{2,1,0:T(8,128)(2,1)}, u32[]{:S(2)}, u32[]{:S(2)}) collective-permute-start(bf16[16,64,256]{2,1,0:T(8,128)(2,1)} %get-tuple-element.191), channel_id=1, source_target_pairs={{0,6},{1,7},{2,4},{3,5},{4,2},{5,3},{6,0},{7,1}} | collective-permute-start | bytes 1572872 | tf_op jit(solution)/shard_map/ppermute | solution.py:297
  960.0 99.3 %collective-permute-start.53 = (bf16[16,64,256]{2,1,0:T(8,128)(2,1)}, bf16[16,64,256]{2,1,0:T(8,128)(2,1)}, u32[]{:S(2)}, u32[]{:S(2)}) collective-permute-start(bf16[16,64,256]{2,1,0:T(8,128)(2,1)} %get-tuple-element.192), channel_id=1, source_target_pairs={{0,7},{1,6},{2,5},{3,4},{4,3},{5,2},{6,1},{7,0}} | collective-permute-start | bytes 1572872 | tf_op jit(solution)/shard_map/ppermute | solution.py:297
  972.6 106.0 %collective-permute-start.79 = (bf16[16,64,256]{2,1,0:T(8,128)(2,1)}, bf16[16,64,256]{2,1,0:T(8,128)(2,1)}, u32[]{:S(2)}, u32[]{:S(2)}) collective-permute-start(bf16[16,64,256]{2,1,0:T(8,128)(2,1)} %get-tuple-element.228), channel_id=1, source_target_pairs={{0,1},{1,0},{2,3},{3,2},{4,5},{5,4},{6,7},{7,6}} | collective-permute-start | bytes 1572872 | tf_op jit(solution)/shard_map/ppermute | solution.py:297
  (101 other events, 3421.9 us)
